TPU v7x, 128 devices: a whole 4x4x4 slice. The times are simulated.
128 devices in a mesh: ctx: 16 (over x, z), head: 8 (over y, core).
Axes of the slice: x: 4, y: 4, z: 4, core: 2. Of those that a mesh axis runs over, the one named last changes fastest.
Arguments:
- input_x_channels: bfloat16 [16384, 8192], P('ctx', 'head'), may hold values from -4 to 4
- input_b_channels: bfloat16 [16384, 1024], P('ctx', 'head'), may hold values from -3 to 3
- input_c_channels: bfloat16 [16384, 1024], P('ctx', 'head'), may hold values from -3 to 3
- input_gate_channels: bfloat16 [16384, 8192], P('ctx', 'head'), may hold values from -75 to 75
- raw_step_sizes: float32 [128, 16384], P('head', 'ctx'), may hold values from -7 to 800
- log_decay_rate: float32 [128], P('head'), may hold values from -8 to -2.3
- head_skip_coeff: float32 [128], P('head'), may hold values from 0.5 to 2
- x_conv_taps: bfloat16 [4, 8192], P(None, 'head'), may hold values from -3 to 3
- b_conv_taps: bfloat16 [4, 1024], P(None, 'head'), may hold values from -3 to 3
- c_conv_taps: bfloat16 [4, 1024], P(None, 'head'), may hold values from -3 to 3
- gated_norm_gain: bfloat16 [8192], P('head'), may hold values from 0.099609375 to 1.8984375
- output_weight: bfloat16 [8192, 4096], P('head'), may hold values from -0.0625 to 0.0625
- adapter_down_panels: bfloat16 [96, 8192, 64], P('ctx', 'head'), may hold values from -0.0625 to 0.0625
- adapter_up_panels: bfloat16 [96, 64, 4096], P('ctx', None, 'head'), may hold values from -0.75 to 0.75
- turn_first_token: int32 [32], replicated, may hold values from 0 to 16256, as said below
- tenant_of_turn: int32 [32], replicated, may hold values from 0 to 95
- tenant_panel_index: int32 [96], replicated, may hold values from 0 to 95, each once
Outputs:
- out: bfloat16 [16384, 4096], P('ctx', 'head')
Inputs may be any that keep to these rules, and one draw needn't show every extreme that they name: `turn_first_token`: strictly increasing multiples of 128; the first is 0; every aligned block of 1024 tokens holds exactly 2 starts, and in every block but the first the earlier of them lies past the block's first token.
All inputs are finite; a program needn't handle non-finite values.
Results may differ from a plain program's by a relative error of at most 0.014.
Values may be sent and summed in bfloat16 or wider, within the bound.
A program may use at most 128 MiB of HBM per device.

v0:
```python
import jax
import jax.numpy as jnp
from jax import lax
from jax.sharding import PartitionSpec as P

P_SIZE = 64
N = 128
K = 4
Q = 128
TURN_DEV = 2


highest = lax.Precision.HIGHEST
epsilon = 1e-05


def shifted(block, axis, distance):
    devices = range(lax.axis_size(axis))
    route = [(i - distance, i) for i in devices if i - distance in devices]
    return lax.ppermute(block, axis, route)


def conv_rows(sequence, tail_rows, weight):
    token_rows = sequence.shape[0]
    joined = jnp.concatenate([tail_rows, sequence], axis=0).astype(jnp.float32)
    total = jnp.zeros((token_rows, sequence.shape[1]), jnp.float32)
    for tap in range(weight.shape[0]):
        total = total + weight[tap].astype(jnp.float32) * joined[tap : tap + token_rows]
    return jax.nn.silu(total).astype(jnp.bfloat16)


def local(
    input_x_channels,
    input_b_channels,
    input_c_channels,
    input_gate_channels,
    raw_step_sizes,
    log_decay_rate,
    head_skip_coeff,
    x_conv_taps,
    b_conv_taps,
    c_conv_taps,
    gated_norm_gain,
    output_weight,
    adapter_down_panels,
    adapter_up_panels,
    turn_first_token,
    tenant_of_turn,
    tenant_panel_index,
):
    token_rows = input_x_channels.shape[0]
    head_count = log_decay_rate.shape[0]
    group_count = input_b_channels.shape[1] // N
    per_group = head_count // group_count
    conv_edge = K - 1
    conv_tails = shifted(
        (
            input_x_channels[token_rows - conv_edge :],
            input_b_channels[token_rows - conv_edge :],
            input_c_channels[token_rows - conv_edge :],
        ),
        "ctx",
        1,
    )
    x_conv = conv_rows(input_x_channels, conv_tails[0], x_conv_taps)
    b_conv = conv_rows(input_b_channels, conv_tails[1], b_conv_taps)
    c_conv = conv_rows(input_c_channels, conv_tails[2], c_conv_taps)
    block_count = token_rows // Q
    step_sizes = jax.nn.softplus(raw_step_sizes)
    decay_rate = jnp.exp(log_decay_rate)
    step_heads = step_sizes.reshape(head_count, block_count, Q)
    running = jnp.cumsum(-step_heads * decay_rate[:, None, None], axis=2)
    run_blocks = running.transpose(1, 0, 2).reshape(block_count, group_count, per_group, Q)
    step_blocks = step_heads.transpose(1, 0, 2).reshape(block_count, group_count, per_group, Q)
    x_blocks = x_conv.astype(jnp.float32).reshape(block_count, Q, group_count, per_group, P_SIZE)
    b_blocks = b_conv.astype(jnp.float32).reshape(block_count, Q, group_count, N)
    c_blocks = c_conv.astype(jnp.float32).reshape(block_count, Q, group_count, N)
    scores = jnp.einsum("cqgn,ckgn->cgqk", c_blocks, b_blocks, precision=highest)
    causal = jnp.arange(Q)[:, None] >= jnp.arange(Q)[None, :]
    log_gap = run_blocks[..., :, None] - run_blocks[..., None, :]
    decay_mat = jnp.where(causal, jnp.exp(jnp.where(causal, log_gap, 0.0)), 0.0)
    mixing = scores[:, :, None] * decay_mat * step_blocks[..., None, :]
    y_local = jnp.einsum("cghqk,ckghp->cqghp", mixing, x_blocks, precision=highest)
    tail_weight = jnp.exp(run_blocks[..., -1:] - run_blocks) * step_blocks
    block_states = jnp.einsum(
        "cghk,ckghp,ckgn->cghpn", tail_weight, x_blocks, b_blocks, precision=highest
    )
    block_log = run_blocks[..., -1]

    def carry_step(carried, inputs):
        fresh_state, step_log = inputs
        return (jnp.exp(step_log)[..., None, None] * carried + fresh_state, carried)

    empty_state = jnp.zeros((group_count, per_group, P_SIZE, N), jnp.float32)
    device_state, before = lax.scan(carry_step, empty_state, (block_states, block_log))
    device_log = jnp.sum(block_log, axis=0)
    run_tokens = run_blocks.transpose(0, 3, 1, 2)
    y_local = y_local + jnp.exp(run_tokens)[..., None] * jnp.einsum(
        "cqgn,cghpn->cqghp", c_blocks, before, precision=highest
    )
    all_logs, states = (
        lax.all_gather(device_log[None], "ctx", axis=0, tiled=True),
        lax.all_gather(device_state[None], "ctx", axis=0, tiled=True),
    )
    device_count = all_logs.shape[0]
    own_index = lax.axis_index("ctx")
    order_index = jnp.arange(device_count)
    between = (order_index[:, None] < order_index[None, :]) & (order_index[None, :] < own_index)
    span_log = jnp.einsum("jk,kgh->jgh", between.astype(jnp.float32), all_logs, precision=highest)
    weights = jnp.where((order_index < own_index)[:, None, None], jnp.exp(span_log), 0.0)
    incoming = jnp.einsum("jgh,jghpn->ghpn", weights, states, precision=highest)
    start_log = jnp.cumsum(block_log, axis=0) - block_log
    device_running = start_log[:, None] + run_tokens
    y_value = y_local + jnp.exp(device_running)[..., None] * jnp.einsum(
        "cqgn,ghpn->cqghp", c_blocks, incoming, precision=highest
    )
    y_value = y_value + head_skip_coeff.reshape(group_count, per_group)[:, :, None] * x_blocks
    group_width = per_group * P_SIZE
    gated = y_value.reshape(token_rows, group_count, group_width) * jax.nn.silu(
        input_gate_channels.astype(jnp.float32)
    ).reshape(token_rows, group_count, group_width)
    norm_scale = lax.rsqrt(jnp.mean(gated * gated, axis=2, keepdims=True) + epsilon)
    y_normed = (
        (gated * norm_scale).reshape(token_rows, -1) * gated_norm_gain.astype(jnp.float32)
    ).astype(jnp.bfloat16)
    own_index = lax.axis_index("ctx")
    slot_count = TURN_DEV + 1
    slot_turns = TURN_DEV * own_index - 1 + jnp.arange(slot_count)
    clipped = jnp.maximum(slot_turns, 0)
    tenants = jnp.take(tenant_of_turn, clipped)
    slot_homes = jnp.take(tenant_panel_index, tenants)
    all_down, all_up = (
        lax.all_gather(adapter_down_panels, "ctx", axis=0, tiled=True),
        lax.all_gather(adapter_up_panels, "ctx", axis=0, tiled=True),
    )
    down_slots = jnp.take(all_down, slot_homes, axis=0)
    up_slots = jnp.take(all_up, slot_homes, axis=0)
    base_out = lax.psum_scatter(
        jnp.dot(y_normed, output_weight, preferred_element_type=jnp.float32).astype(jnp.bfloat16),
        "head",
        scatter_dimension=1,
        tiled=True,
    ).astype(jnp.float32)
    own_starts = lax.dynamic_slice_in_dim(turn_first_token, TURN_DEV * own_index, TURN_DEV, 0)
    token_place = own_index * token_rows + jnp.arange(token_rows)
    token_slot = jnp.sum((token_place[:, None] >= own_starts[None, :]).astype(jnp.int32), axis=1)
    slot_mask = (token_slot[:, None] == jnp.arange(slot_count)[None, :]).astype(jnp.float32)
    low_slots = jnp.einsum("tc,scr->tsr", y_normed, down_slots, preferred_element_type=jnp.float32)
    rank_reduced = jnp.sum(low_slots * slot_mask[:, :, None], axis=1)
    rank_reduced = lax.psum(rank_reduced, "head").astype(jnp.bfloat16)
    adapter_out = jnp.einsum(
        "tr,srd->tsd", rank_reduced, up_slots, preferred_element_type=jnp.float32
    )
    adapter_out = jnp.sum(adapter_out * slot_mask[:, :, None], axis=1)
    return (base_out + adapter_out).astype(jnp.bfloat16)


def solution(mesh):
    in_specs = (
        P("ctx", "head"),
        P("ctx", "head"),
        P("ctx", "head"),
        P("ctx", "head"),
        P("head", "ctx"),
        P("head"),
        P("head"),
        P(None, "head"),
        P(None, "head"),
        P(None, "head"),
        P("head"),
        P("head", None),
        P("ctx", "head", None),
        P("ctx", None, "head"),
        P(),
        P(),
        P(),
    )
    out_specs = P("ctx", "head")
    return jax.shard_map(local, mesh=mesh, in_specs=in_specs, out_specs=out_specs, check_vma=False)
```

profile of v0, /device:TPU:0, one launch (start us, length us, event | category | flops | bytes accessed | tf_op | source)
XLA Modules:
  0.0 349.8 jit_solution(5705735439827553091)
XLA Ops:
  8.2 3.9 %collective-permute-start = (bf16[3,1024]{0,1:T(8,128)(2,1)}, bf16[3,1024]{0,1:T(8,128)(2,1)S(1)}, u32[]{:S(2)}, u32[]{:S(2)}) collective-permute-start(bf16[3,1024]{0,1:T(8,128)(2,1)} %copy.74), channel_id=1, source_target_pairs={{0,8},{8,16},{16,24},{24,32},{32,40},{40,48},{48,56},{56,64},{64,7... | collective-permute-start | bytes 18440 | tf_op jit(solution)/shard_map/ppermute | solution.py:20
  12.8 3.8 %collective-permute-start.2 = (bf16[3,128]{1,0:T(4,128)(2,1)S(1)}, bf16[3,128]{1,0:T(4,128)(2,1)S(1)}, u32[]{:S(2)}, u32[]{:S(2)}) collective-permute-start(bf16[3,128]{1,0:T(4,128)(2,1)S(1)} %slice.104), channel_id=1, source_target_pairs={{0,8},{8,16},{16,24},{24,32},{32,40},{40,48},{48,56},{56,64},{64,7... | collective-permute-start | bytes 2312 | tf_op jit(solution)/shard_map/ppermute | solution.py:20
  19.1 4.5 %reduce_window_sum.22 = f32[16,8,128]{2,1,0:T(8,128)S(1)} reduce-window(f32[16,8,128]{2,1,0:T(8,128)S(1)} %negate_multiply_fusion, f32[]{:T(128)} %constant.95.clone.1), window={size=1x1x128 pad=0_0x0_0x127_0}, to_apply=%region_0.1 | reduce-window | flops 2080768 | bytes 131076 | tf_op jit(solution)/shard_map/jit(cumsum)/reduce_window_sum | solution.py:72
  25.0 2.9 copy.75
  28.5 1.2 maximum_convert_fusion
  29.7 5.5 %convert_bitcast_fusion = (f32[128,8,8,128]{3,1,2,0:T(8,128)}, bf16[1024,1024]{0,1:T(8,128)(2,1)S(1)}) fusion(f32[1027,1024]{0,1:T(8,128)S(1)} %maximum_convert_fusion, f32[1024]{0:T(1024)S(1)} %bitcast.186, f32[1024]{0:T(1024)S(1)} %bitcast.187, f32[1024]{0:T(1024)S(1)} %bitcast.185, f32[1024]{0:T(1024)S(1)} %bitcast.184), kind=kLoop, calls=%fused_computation.43 | loop fusion | flops 13631488 | bytes 23085056
  36.2 3.8 %fusion.31 = f32[8,1,16,64,128]{4,3,2,1,0:T(8,128)} fusion(bf16[8,128,128,1]{2,1,3,0:T(8,128)(2,1)S(1)} %bitcast.173, f32[8,128,16,64]{1,0,3,2:T(8,128)S(1)} %convert_multiply_fusion.1), kind=kOutput, calls=%fused_computation.55 | convolution fusion | flops 1610612736 | bytes 8650752 | tf_op jit(solution)/shard_map/cghk,ckghp,ckgn->cghpn/dot_general | solution.py:85
  40.0 16.3 %while.13 = (s32[]{:T(128)}, f32[1,16,64,128]{3,2,1,0:T(8,128)S(1)}, f32[8,1,16,64,128]{4,3,2,1,0:T(8,128)}, f32[8,1,16]{2,1,0:T(1,128)S(1)}, f32[8,1,16,64,128]{4,3,2,1,0:T(8,128)}, /*index=5*/s32[]{:T(128)}, s32[]{:T(128)}) while((s32[]{:T(128)}, f32[1,16,64,128]{3,2,1,0:T(8,128)S(1)}, f32[8,1,16,64,128]{4,3,2,1,0:T(8,128)}, ...), condition=%wide.region_2.3_spmd.clone, body=%wide.region_1.2_spmd.clone.sunk | while | flops 524291 | bytes 2622240 | solution.py:95
  40.9 1.2 bitcast_add_fusion.2
  51.1 1.2 bitcast_add_fusion.2
  58.7 3.5 %collective-permute-start.1 = (bf16[3,128]{1,0:T(4,128)(2,1)S(1)}, bf16[3,128]{1,0:T(4,128)(2,1)S(1)}, u32[]{:S(2)}, u32[]{:S(2)}) collective-permute-start(bf16[3,128]{1,0:T(4,128)(2,1)S(1)} %slice.95), channel_id=1, source_target_pairs={{0,8},{8,16},{16,24},{24,32},{32,40},{40,48},{48,56},{56,64},{64,7... | collective-permute-start | bytes 2312 | tf_op jit(solution)/shard_map/ppermute | solution.py:20
  63.9 36.2 %all-reduce = f32[256]{0:T(256)S(1)} all-reduce(f32[256]{0:T(256)S(1)} %dynamic-update-slice), channel_id=2, replica_groups=mesh['ctx'=16,'head'=8] {'ctx'}, use_global_device_ids=true, to_apply=%add | all-reduce | flops 256 | bytes 2048
  100.7 4.0 %copy.92 = bf16[1024,1024]{0,1:T(8,128)(2,1)} copy(bf16[1024,1024]{1,0:T(8,128)(2,1)} %param.22) | data formatting | bytes 4194304 | tf_op args[3]
  105.4 1.5 copy-done.3
  106.9 3.0 copy.104
  110.1 3.5 %fusion.21 = f32[8,16,64,128]{3,2,1,0:T(8,128)} fusion(bf16[8,128,128,1]{2,1,3,0:T(8,128)(2,1)S(1)} %bitcast.170, f32[8,1,16,64,128]{4,3,2,1,0:T(8,128)S(1)} %copy-done.8), kind=kOutput, calls=%fused_computation.38 | convolution fusion | flops 1610612736 | bytes 8650752 | tf_op jit(solution)/shard_map/cqgn,cghpn->cqghp/dot_general | solution.py:98
  113.6 11.3 %fusion.4 = f32[8,16,64,128]{3,2,1,0:T(8,128)} fusion(f32[8,16,128]{2,1,0:T(8,128)S(1)} %copy.78, f32[8,16,128]{2,1,0:T(8,128)S(1)} %copy.76, f32[8,128,128]{2,1,0:T(8,128)S(1)} %fusion.61, pred[128,128]{1,0:T(8,128)(4,1)S(1)} %iota_compare_fusion, bf16[8,128,16,64]{1,0,3,2:T(8,128)(2,1)S(1)} %bitcast.167), kind=kOutput, calls=%fused_computation.11 | convolution fusion | flops 1621098496 | bytes 6963200 | tf_op jit(solution)/shard_map/cghqk,ckghp->cqghp/dot_general | solution.py:83
  124.9 3.8 %all-gather.10.cloned.1.call-done = f32[16,16,64,128]{3,2,1,0:T(8,128)} async-done(((f32[1,16,64,128]{3,2,1,0:T(8,128)}), f32[16,16,64,128]{3,2,1,0:T(8,128)}) %all-gather.10.cloned.1.call-update) | async-done | bytes 8388624 | tf_op jit(solution)/shard_map/all_gather | solution.py:103
  128.7 12.8 %fusion.2 = f32[16,1,64,128]{3,1,2,0:T(1,128)S(1)} fusion(f32[16,16,1,1]{0,2,3,1:T(1,128)S(1)} %copy.96, f32[16,16,64,128]{3,2,1,0:T(8,128)} %all-gather.10.cloned.1.call-done), kind=kOutput, calls=%fused_computation.9 | convolution fusion | flops 25165824 | bytes 8913920 | tf_op jit(solution)/shard_map/jgh,jghpn->ghpn/dot_general | solution.py:111
  141.5 5.1 %fusion.19 = f32[8,128,1,16,64]{1,4,3,0,2:T(8,128)S(1)} fusion(f32[8,16,64,128]{3,2,1,0:T(8,128)S(1)} %copy-done.6, f32[8,16,64,128]{3,2,1,0:T(8,128)} %fusion.4, f32[8,128,1,16,64]{1,0,4,3,2:T(8,128)S(1)} %bitcast.164, f32[16,64,128,1]{2,1,0,3:T(8,128)S(1)} %bitcast.175, bf16[8,128,128,1]{2,1,3,0:T(8,128)(2,1)S(1)} %bitcast.171, f32[16]{0:T(128)S(1)} %copy-done.13, ...), kind=kOutput, calls=%fused_computation.35 | convolution fusion | flops 1616904192 | bytes 17694784 | tf_op jit(solution)/shard_map/cqgn,ghpn->cqghp/dot_general | solution.py:114
  146.6 3.3 copy.91
  150.0 1.7 multiply_reduce_fusion.1
  151.8 2.0 copy-done.4
  153.8 11.5 %convolution_convert_fusion = bf16[1024,4096]{1,0:T(8,128)(2,1)} fusion(bf16[1024,4096]{1,0:T(8,128)(2,1)S(1)} %bitcast.189, f32[1024,1024]{0,1:T(8,128)S(1)} %get-tuple-element.84, f32[1024]{0:T(1024)S(1)} %convert_element_type.84, f32[1024]{0:T(1024)S(1)} %add_rsqrt_fusion), kind=kOutput, calls=%fused_computation.18 | convolution fusion | flops 8597274624 | bytes 20979712 | tf_op jit(solution)/shard_map/dot_general | solution.py:139
  166.9 24.9 %all-gather.8.cloned.1.call-done = bf16[96,64,512]{2,1,0:T(8,128)(2,1)} async-done(((bf16[6,64,512]{2,1,0:T(8,128)(2,1)}), bf16[96,64,512]{2,1,0:T(8,128)(2,1)}) %all-gather.8.cloned.1.call-update) | async-done | bytes 6291472 | tf_op jit(solution)/shard_map/all_gather | solution.py:134
  191.8 3.3 gather_fusion.3
  195.1 88.6 %all-gather.6.cloned.1.call-done = bf16[96,1024,64]{1,2,0:T(8,128)(2,1)} async-done(((bf16[6,1024,64]{1,2,0:T(8,128)(2,1)}), bf16[96,1024,64]{1,2,0:T(8,128)(2,1)}) %all-gather.6.cloned.1.call-update) | async-done | bytes 12582928 | tf_op jit(solution)/shard_map/all_gather | solution.py:133
  283.7 5.1 %gather_fusion.2 = bf16[3,1024,64]{1,2,0:T(8,128)(2,1)S(1)} fusion(bf16[96,1024,64]{1,2,0:T(8,128)(2,1)} %all-gather.6.cloned.1.call-done, s32[1024]{0:T(1024)S(1)} %pad_clamp_fusion), kind=kCustom, calls=%fused_computation.2 | custom fusion | bytes 786444 | tf_op jit(solution)/shard_map/jit(_take)/gather | solution.py:136
  289.0 2.9 fusion.59
  291.9 31.3 %all-reduce.2 = bf16[1024,64]{0,1:T(8,128)(2,1)S(1)} all-reduce(f32[1024,64]{0,1:T(8,128)S(1)} %multiply_reduce_fusion.2), channel_id=1, replica_groups=mesh['ctx'=16,'head'=8] {'head'}, use_global_device_ids=true, to_apply=%region_9.10 | all-reduce | flops 65536 | bytes 393216 | tf_op jit(solution)/shard_map/psum | solution.py:150
  324.3 16.4 %reduce-scatter.2.cloned.1.call-done = bf16[1024,512]{1,0:T(8,128)(2,1)} async-done(((bf16[1024,4096]{1,0:T(8,128)(2,1)}), bf16[1024,512]{1,0:T(8,128)(2,1)}) %reduce-scatter.2.cloned.1.call-update) | async-done | bytes 1048592 | tf_op jit(solution)/shard_map/reduce_scatter | solution.py:138
  340.7 2.6 add_convert_fusion
  (126 shorter events, 29.0 us)
Async XLA Ops:
  6.5 158.8 %copy-start = (s32[32]{0:T(128)S(1)}, s32[32]{0:T(128)}, u32[]{:S(2)}) copy-start(s32[32]{0:T(128)} %param.34) | copy-start | bytes 388
  6.5 21.5 %copy-start.9 = (bf16[1024,128]{1,0:T(8,128)(2,1)S(1)}, bf16[1024,128]{1,0:T(8,128)(2,1)}, u32[]{:S(2)}) copy-start(bf16[1024,128]{1,0:T(8,128)(2,1)} %param.20) | copy-start | bytes 786436
  6.5 122.1 %all-gather.10.cloned.1.call-start = ((), (), s32[]{:S(2)}) async-start(), calls=%async_computation.4 | async-start | bytes 8912896 | tf_op jit(solution)/shard_map/all_gather | solution.py:103
  8.2 20.3 %collective-permute-start = (bf16[3,1024]{0,1:T(8,128)(2,1)}, bf16[3,1024]{0,1:T(8,128)(2,1)S(1)}, u32[]{:S(2)}, u32[]{:S(2)}) collective-permute-start(bf16[3,1024]{0,1:T(8,128)(2,1)} %copy.74), channel_id=1, source_target_pairs={{0,8},{8,16},{16,24},{24,32},{32,40},{40,48},{48,56},{56,64},{64,7... | collective-permute-start | bytes 18440 | tf_op jit(solution)/shard_map/ppermute | solution.py:20
  12.8 15.2 %collective-permute-start.2 = (bf16[3,128]{1,0:T(4,128)(2,1)S(1)}, bf16[3,128]{1,0:T(4,128)(2,1)S(1)}, u32[]{:S(2)}, u32[]{:S(2)}) collective-permute-start(bf16[3,128]{1,0:T(4,128)(2,1)S(1)} %slice.104), channel_id=1, source_target_pairs={{0,8},{8,16},{16,24},{24,32},{32,40},{40,48},{48,56},{56,64},{64,7... | collective-permute-start | bytes 2312 | tf_op jit(solution)/shard_map/ppermute | solution.py:20
  40.0 18.7 %copy-start.10 = (bf16[1024,128]{1,0:T(8,128)(2,1)S(1)}, bf16[1024,128]{1,0:T(8,128)(2,1)}, u32[]{:S(2)}) copy-start(bf16[1024,128]{1,0:T(8,128)(2,1)} %param.21) | copy-start | bytes 786436
  40.0 22.2 %copy-start.15 = (u32[128]{0:T(128)S(1)}, u32[128]{0:T(128)}, u32[]{:S(2)}) copy-start(u32[128]{0:T(128)} %constant.114) | copy-start | bytes 1540
  40.0 60.3 %copy-start.11 = (bf16[4,128]{1,0:T(4,128)(2,1)S(1)}, bf16[4,128]{1,0:T(4,128)(2,1)}, u32[]{:S(2)}) copy-start(bf16[4,128]{1,0:T(4,128)(2,1)} %param.28) | copy-start | bytes 3076
  56.3 0.8 copy-start.2
  56.3 48.3 %copy-start.12 = (bf16[1024]{0:T(1024)(128)(2,1)S(1)}, bf16[1024]{0:T(1024)(128)(2,1)}, u32[]{:S(2)}) copy-start(bf16[1024]{0:T(1024)(128)(2,1)} %param.29) | copy-start | bytes 6148
  57.1 134.6 %all-gather.8.cloned.1.call-start = ((), (), s32[]{:S(2)}) async-start(), calls=%async_computation.3 | async-start | bytes 6684672 | tf_op jit(solution)/shard_map/all_gather | solution.py:134
  57.9 225.8 %all-gather.6.cloned.1.call-start = ((), (), s32[]{:S(2)}) async-start(), calls=%async_computation.2 | async-start | bytes 13369344 | tf_op jit(solution)/shard_map/all_gather | solution.py:133
  58.6 282.1 %reduce-scatter.2.cloned.1.call-start = ((), (), s32[]{:S(2)}) async-start(), calls=%async_computation.1 | async-start | bytes 9437184 | tf_op jit(solution)/shard_map/reduce_scatter | solution.py:138
  58.7 46.0 %collective-permute-start.1 = (bf16[3,128]{1,0:T(4,128)(2,1)S(1)}, bf16[3,128]{1,0:T(4,128)(2,1)S(1)}, u32[]{:S(2)}, u32[]{:S(2)}) collective-permute-start(bf16[3,128]{1,0:T(4,128)(2,1)S(1)} %slice.95), channel_id=1, source_target_pairs={{0,8},{8,16},{16,24},{24,32},{32,40},{40,48},{48,56},{56,64},{64,7... | collective-permute-start | bytes 2312 | tf_op jit(solution)/shard_map/ppermute | solution.py:20
  104.6 2.2 copy-start.3
  106.9 3.2 copy-start.8
  124.9 16.7 %copy-start.13 = (f32[16]{0:T(128)S(1)}, f32[16]{0:T(128)}, u32[]{:S(2)}) copy-start(f32[16]{0:T(128)} %param.25) | copy-start | bytes 196
  128.7 12.9 %copy-start.5 = (f32[128,8,8,128]{3,2,1,0:T(8,128)S(1)}, f32[128,8,8,128]{3,2,1,0:T(8,128)}, u32[]{:S(2)}) copy-start(f32[128,8,8,128]{3,2,1,0:T(8,128)} %copy.104) | copy-start | bytes 12582916
  128.7 12.9 %copy-start.6 = (f32[8,16,64,128]{3,2,1,0:T(8,128)S(1)}, f32[8,16,64,128]{3,2,1,0:T(8,128)}, u32[]{:S(2)}) copy-start(f32[8,16,64,128]{3,2,1,0:T(8,128)} %fusion.21) | copy-start | bytes 12582916
  146.6 3.3 copy-start.7
  146.6 7.2 %slice-start = ((s8[8388608]{0:T(1024)(128)(4,1)}), s8[4194304]{0:T(1024)(128)(4,1)S(1)}, s32[]{:S(2)}) async-start(s8[8388608]{0:T(1024)(128)(4,1)} %bitcast.188), calls=%async_computation.5 | async-start | bytes 8388608
  150.0 3.8 %slice-start.1 = ((s8[8388608]{0:T(1024)(128)(4,1)}), s8[4194304]{0:T(1024)(128)(4,1)S(1)}, s32[]{:S(2)}) async-start(s8[8388608]{0:T(1024)(128)(4,1)} %bitcast.188), calls=%async_computation.6 | async-start | bytes 8388608
  151.7 2.0 copy-start.4
  165.3 0.7 copy-start.1
  165.3 1.4 copy-start.14
Sparse Core Ops, SparseCore 0:
  57.3 71.3 all-gather.9
  130.8 60.8 all-gather.7
  194.0 89.7 all-gather.5
  286.0 54.6 reduce-scatter.1
where the time goes:
time: 351 us; the launch traced here: 350 us
  waiting for transfers between devices  135 us (38%)
  blocking collectives  67.5 us (19%)
  matrix products  52.3 us (15%)
  other arithmetic  36.4 us (10%)
  local copies, waits for them, and re-layouts  32.7 us (9%)
  between operations  14.3 us (4%)
  starting transfers between devices  11.4 us (3%)
    all_gather x1, waiting for transfers between devices, local(): lax.all_gather(adapter_down_panels, 'ctx', axis=0, tiled=True)  88.6 us
    unnamed x1, blocking collectives  36.2 us
    psum x1, blocking collectives, local(): rank_reduced = lax.psum(rank_reduced, 'head').astype(jnp.bfloat16)  31.3 us
    all_gather x1, waiting for transfers between devices, local(): lax.all_gather(adapter_up_panels, 'ctx', axis=0, tiled=True)  24.9 us
    reduce_scatter x1, waiting for transfers between devices, local(): lax.psum_scatter(jnp.dot(y_normed, output_weight, preferred_element_type=...  16.4 us
    unnamed x44, local copies, waits for them, and re-layouts  15.9 us
    dot_general x1, matrix products, local(): incoming = jnp.einsum('jgh,jghpn->ghpn', weights, states, precision=highest)  12.8 us
    dot_general x1, matrix products, local(): jnp.dot(y_normed, output_weight, preferred_element_type=jnp.float32)  11.5 us
  transfers between devices with their start and end apart: 7, of which 4 were waited for; matrix products, arithmetic and copies ran while one was open for 24% of the time, Pallas kernels for 0%

commit v1 on v0

v1 whole, which is shorter than its diff:
```python
import functools

import jax
import jax.numpy as jnp
from jax import lax
from jax.experimental import pallas as pl
from jax.experimental.pallas import tpu as pltpu
from jax.sharding import PartitionSpec as P

P_SIZE = 64
N = 128
Q = 128
TURN_DEV = 2
LOG2E = 1.4426950408889634
EPSILON = 1e-05
VMEM_LIMIT = 60 * 1024 * 1024
MESH = pl.DeviceIdType.MESH
F32 = jnp.float32
BF16 = jnp.bfloat16


def silu(v):
    half = 0.5 * v
    return half + half * jnp.tanh(half)


def dot(a, b):
    return jnp.dot(a, b, preferred_element_type=F32)


def dot_dims(a, b, ca, cb):
    return lax.dot_general(a, b, (((ca,), (cb,)), ((), ())), preferred_element_type=F32)


def scan_kernel(
    rate_ref, skip_ref, x_ref, b_ref, c_ref, z_ref, raw_ref, halo_ref, xt_ref, bt_ref, ct_ref,
    ylg_ref, eg_ref, cc_ref, s_ref, d_ref,
    xp, bp, cp, start, skl,
):
    step = pl.program_id(0)
    heads = raw_ref.shape[0]
    width = x_ref.shape[1]
    lane = lax.broadcasted_iota(jnp.int32, (8, 128), 1)

    @pl.when(step == 0)
    def _():
        xp[0:8, :] = halo_ref[:, 0:width].astype(F32)
        bp[0:8, :] = halo_ref[:, width : width + N].astype(F32)
        cp[0:8, :] = halo_ref[:, width + N : width + 2 * N].astype(F32)
        start[...] = jnp.zeros_like(start)
        s_ref[...] = jnp.zeros_like(s_ref)
        for pair in range(heads // 2):
            skl[:, pair * 128 : pair * 128 + 128] = jnp.where(
                lane < P_SIZE, skip_ref[2 * pair], skip_ref[2 * pair + 1]
            )

    @pl.when(step > 0)
    def _():
        xp[0:8, :] = xp[Q : Q + 8, :]
        bp[0:8, :] = bp[Q : Q + 8, :]
        cp[0:8, :] = cp[Q : Q + 8, :]

    xp[8 : 8 + Q, :] = x_ref[...].astype(F32)
    bp[8 : 8 + Q, :] = b_ref[...].astype(F32)
    cp[8 : 8 + Q, :] = c_ref[...].astype(F32)

    def conv(padded, taps, sl):
        total = taps[0:1, sl].astype(F32) * padded[5 : 5 + Q, sl]
        for k in range(1, 4):
            total = total + taps[k : k + 1, sl].astype(F32) * padded[5 + k : 5 + k + Q, sl]
        return silu(total).astype(BF16)

    every = slice(0, N)
    bc = conv(bp, bt_ref, every)
    cc = conv(cp, ct_ref, every)
    cc_ref[...] = cc
    bt = bc.astype(F32).T.astype(BF16)
    row = lax.broadcasted_iota(jnp.int32, (Q, Q), 0)
    col = lax.broadcasted_iota(jnp.int32, (Q, Q), 1)
    scores = jnp.where(row >= col, dot(cc, bt), 0.0)

    raw = raw_ref[...]
    dt = jnp.maximum(raw, 0.0) + jnp.log1p(jnp.exp(-jnp.abs(raw)))
    hrow = lax.broadcasted_iota(jnp.int32, (heads, Q), 0)
    lrow = lax.broadcasted_iota(jnp.int32, (heads, Q), 1)
    rate = jnp.zeros((heads, Q), F32)
    for h in range(heads):
        rate = jnp.where(hrow == h, rate_ref[h], rate)
    run = -dt * jnp.exp(rate)
    shift = 1
    while shift < Q:
        run = run + jnp.where(lrow >= shift, pltpu.roll(run, shift, 1), 0.0)
        shift *= 2
    run2 = run * LOG2E
    last2 = jnp.broadcast_to(run2[:, Q - 1 : Q], (heads, Q))
    stacked = jnp.concatenate(
        [dt, run2] + [jnp.zeros((heads, Q), F32)] * ((Q - 2 * heads) // heads), axis=0
    )
    tr = stacked.T
    before2 = start[...]
    start[...] = before2 + last2
    half_lane = lax.broadcasted_iota(jnp.int32, (Q, 128), 1) < P_SIZE
    half_row = lax.broadcasted_iota(jnp.int32, (1, 128), 1) < P_SIZE

    for pair in range(heads // 2):
        h0, h1 = 2 * pair, 2 * pair + 1
        sl = slice(pair * 128, pair * 128 + 128)
        xc = conv(xp, xt_ref, sl).astype(F32)
        dt_e = jnp.where(half_lane, tr[:, h0 : h0 + 1], tr[:, h1 : h1 + 1])
        c0 = jnp.broadcast_to(tr[:, heads + h0 : heads + h0 + 1], (Q, Q))
        c1 = jnp.broadcast_to(tr[:, heads + h1 : heads + h1 + 1], (Q, Q))
        run_e = jnp.where(half_lane, c0, c1)
        last_e = jnp.where(half_row, last2[h0 : h0 + 1, :], last2[h1 : h1 + 1, :])
        start_e = jnp.where(half_row, before2[h0 : h0 + 1, :], before2[h1 : h1 + 1, :])
        xdt = xc * dt_e
        m0 = (scores * jnp.exp2(jnp.minimum(c0 - run2[h0 : h0 + 1, :], 0.0))).astype(BF16)
        m1 = (scores * jnp.exp2(jnp.minimum(c1 - run2[h1 : h1 + 1, :], 0.0))).astype(BF16)
        mixing = jnp.concatenate([m0, m1], axis=1)
        xdt_pair = jnp.concatenate(
            [jnp.where(half_lane, xdt, 0.0), jnp.where(half_lane, 0.0, xdt)], axis=0
        ).astype(BF16)
        grow = jnp.exp2(run_e)
        carried = s_ref[:, sl]
        y = dot(mixing, xdt_pair) + grow * dot(cc, carried.astype(BF16)) + skl[0:1, sl] * xc
        gate = silu(z_ref[:, sl].astype(F32))
        ylg_ref[:, sl] = (y * gate).astype(BF16)
        eg_ref[:, sl] = (grow * jnp.exp2(start_e) * gate).astype(BF16)
        weighted = (xdt * jnp.exp2(last_e - run_e)).astype(BF16)
        s_ref[:, sl] = jnp.exp2(last_e) * carried + dot(bt, weighted)
        d_ref[:, sl] = jnp.broadcast_to(jnp.exp2(start_e + last_e), (8, 128))


def local_scan(x, b, c, z, raw, rate, skip, halo, xt, bt, ct):
    tokens, width = x.shape
    heads = raw.shape[0]
    smem = pl.BlockSpec(memory_space=pltpu.SMEM)
    whole = lambda a: pl.BlockSpec(a.shape, lambda i: (0,) * a.ndim)
    rows = lambda w: pl.BlockSpec((Q, w), lambda i: (i, 0))
    return pl.pallas_call(
        scan_kernel,
        grid=(tokens // Q,),
        in_specs=[
            smem, smem, rows(width), rows(N), rows(N), rows(width),
            pl.BlockSpec((heads, Q), lambda i: (0, i)),
            whole(halo), whole(xt), whole(bt), whole(ct),
        ],
        out_specs=[
            rows(width), rows(width), rows(N),
            pl.BlockSpec((N, width), lambda i: (0, 0)),
            pl.BlockSpec((8, width), lambda i: (0, 0)),
        ],
        out_shape=[
            jax.ShapeDtypeStruct((tokens, width), BF16),
            jax.ShapeDtypeStruct((tokens, width), BF16),
            jax.ShapeDtypeStruct((tokens, N), BF16),
            jax.ShapeDtypeStruct((N, width), F32),
            jax.ShapeDtypeStruct((8, width), F32),
        ],
        scratch_shapes=[
            pltpu.VMEM((Q + 8, width), F32),
            pltpu.VMEM((Q + 8, N), F32),
            pltpu.VMEM((Q + 8, N), F32),
            pltpu.VMEM((heads, Q), F32),
            pltpu.VMEM((8, width), F32),
        ],
        compiler_params=pltpu.CompilerParams(
            dimension_semantics=("arbitrary",), vmem_limit_bytes=VMEM_LIMIT
        ),
        name="local_scan",
    )(rate, skip, x, b, c, z, raw, halo, xt, bt, ct)


def partners():
    me = lax.axis_index("ctx")
    x, z = me // 4, me % 4
    return [
        (x * 4 + (z + 1 - 2 * (z % 2)), z % 2),
        (x * 4 + (3 - z), z // 2),
        ((x + 1 - 2 * (x % 2)) * 4 + z, x % 2),
        ((3 - x) * 4 + z, x // 2),
    ]


def exchange_kernel(
    s_ref, d_ref, inc_ref, total, prefix, decay, dsend, drecv, ssend, srecv,
    sem_ds, sem_dr, sem_ss, sem_sr, *, chunks,
):
    steps = partners()
    barrier = pltpu.get_barrier_semaphore()
    for other, _ in steps:
        pl.semaphore_signal(barrier, inc=1, device_id={"ctx": other}, device_id_type=MESH)
    width = s_ref.shape[1]
    cw = width // chunks

    def state_copy(c, s):
        return pltpu.make_async_remote_copy(
            src_ref=ssend.at[s, c], dst_ref=srecv.at[s, c],
            send_sem=sem_ss.at[s, c], recv_sem=sem_sr.at[s, c],
            device_id={"ctx": steps[s][0]}, device_id_type=MESH,
        )

    def decay_copy(s):
        return pltpu.make_async_remote_copy(
            src_ref=dsend.at[s], dst_ref=drecv.at[s],
            send_sem=sem_ds.at[s], recv_sem=sem_dr.at[s],
            device_id={"ctx": steps[s][0]}, device_id_type=MESH,
        )

    for c in range(chunks):
        ssend[0, c] = s_ref[:, c * cw : c * cw + cw].astype(BF16)
    dsend[0] = d_ref[...]
    total[...] = s_ref[...]
    prefix[...] = jnp.zeros_like(prefix)
    pl.semaphore_wait(barrier, len(steps))
    decay_copy(0).start()
    for c in range(chunks):
        state_copy(c, 0).start()
    decay[0] = d_ref[...]
    decay[1] = jnp.ones_like(d_ref)
    for wave in range(chunks + 3):
        for s in range(4):
            c = wave - s
            if c < 0 or c >= chunks:
                continue
            sl = slice(c * cw, c * cw + cw)
            upper = steps[s][1] == 1
            if c == 0:
                decay_copy(s).wait_recv()
                theirs = drecv[s]
                decay[2 * s + 2] = decay[2 * s] * theirs
                decay[2 * s + 3] = decay[2 * s + 1] * jnp.where(upper, theirs, 1.0)
                if s < 3:
                    dsend[s + 1] = decay[2 * s + 2]
                    decay_copy(s + 1).start()
            state_copy(c, s).wait_recv()
            incoming = srecv[s, c].astype(F32)
            mine = decay[2 * s, 0:1, sl]
            ahead = decay[2 * s + 1, 0:1, sl]
            theirs = drecv[s, 0:1, sl]
            prefix[:, sl] = prefix[:, sl] + jnp.where(upper, ahead, 0.0) * incoming
            if s < 3:
                new = (
                    jnp.where(upper, mine, 1.0) * incoming
                    + jnp.where(upper, 1.0, theirs) * total[:, sl]
                )
                total[:, sl] = new
                ssend[s + 1, c] = new.astype(BF16)
                state_copy(c, s + 1).start()
    inc_ref[...] = prefix[...].astype(BF16)
    for s in range(4):
        decay_copy(s).wait_send()
        for c in range(chunks):
            state_copy(c, s).wait_send()


def exchange(state, decay, chunks=8):
    width = state.shape[1]
    cw = width // chunks
    vmem = pl.BlockSpec(memory_space=pltpu.VMEM)
    return pl.pallas_call(
        functools.partial(exchange_kernel, chunks=chunks),
        in_specs=[vmem, vmem],
        out_specs=vmem,
        out_shape=jax.ShapeDtypeStruct((N, width), BF16),
        scratch_shapes=[
            pltpu.VMEM((N, width), F32),
            pltpu.VMEM((N, width), F32),
            pltpu.VMEM((10, 8, width), F32),
            pltpu.VMEM((4, 8, width), F32),
            pltpu.VMEM((4, 8, width), F32),
            pltpu.VMEM((4, chunks, N, cw), BF16),
            pltpu.VMEM((4, chunks, N, cw), BF16),
            pltpu.SemaphoreType.DMA((4,)),
            pltpu.SemaphoreType.DMA((4,)),
            pltpu.SemaphoreType.DMA((4, chunks)),
            pltpu.SemaphoreType.DMA((4, chunks)),
        ],
        compiler_params=pltpu.CompilerParams(
            collective_id=1, has_side_effects=True, vmem_limit_bytes=VMEM_LIMIT
        ),
        name="state_exchange",
    )(state, decay)


LAG = (1, 2, 3, 4)


def project_kernel(
    slot_ref, ylg_ref, eg_ref, cc_ref, inc_ref, gain_ref, down_ref, w_ref,
    base_ref, low_ref,
    wv, own, psend, precv, rsend, rrecv, lsend, lrecv, lout,
    sem_w, sem_ps, sem_pr, sem_rs, sem_rr, sem_ls, sem_lr, sem_as, sem_ar,
):
    head = lax.axis_index("head")
    y, core = head // 2, head % 2
    blocks = ylg_ref.shape[0] // Q
    feat = base_ref.shape[1]
    half = Q // 2
    barrier = pltpu.get_barrier_semaphore()
    for k in range(1, 8):
        pl.semaphore_signal(
            barrier, inc=1, device_id={"head": (head + k) % 8}, device_id_type=MESH
        )

    dests = [(y + 3) % 4, (y + 1) % 4, (y + 2) % 4, y]

    def w_copy(d, side):
        index = d * 2 + side
        at = pl.multiple_of(index * feat, feat)
        return pltpu.make_async_copy(w_ref.at[:, pl.ds(at, feat)], wv.at[index], sem_w.at[index])

    for d in dests:
        for side in (1 - core, core):
            w_copy(d, side).start()

    def pair_copy(b, d):
        return pltpu.make_async_remote_copy(
            src_ref=psend.at[b, d], dst_ref=precv.at[b, d],
            send_sem=sem_ps.at[b, d], recv_sem=sem_pr.at[b, d],
            device_id={"head": y * 2 + 1 - core}, device_id_type=MESH,
        )

    def ring_copy(b, j, way):
        to = (y + 1 + 2 * way) % 4
        return pltpu.make_async_remote_copy(
            src_ref=rsend.at[b, j, way], dst_ref=rrecv.at[b, j, way],
            send_sem=sem_rs.at[b, j, way], recv_sem=sem_rr.at[b, j, way],
            device_id={"head": to * 2 + core}, device_id_type=MESH,
        )

    def low_copy(b):
        return pltpu.make_async_remote_copy(
            src_ref=lsend.at[b], dst_ref=lrecv.at[head],
            send_sem=sem_ls.at[b], recv_sem=sem_lr.at[head],
            device_id={"head": b}, device_id_type=MESH,
        )

    def low_arrival(k):
        return pltpu.make_async_remote_copy(
            src_ref=lsend.at[k], dst_ref=lrecv.at[k],
            send_sem=sem_ls.at[k], recv_sem=sem_lr.at[k],
            device_id={"head": k}, device_id_type=MESH,
        )

    def sum_copy(k):
        return pltpu.make_async_remote_copy(
            src_ref=lout.at[head], dst_ref=lout.at[head],
            send_sem=sem_as.at[k], recv_sem=sem_ar.at[head],
            device_id={"head": k}, device_id_type=MESH,
        )

    def sum_arrival(k):
        return pltpu.make_async_remote_copy(
            src_ref=lout.at[k], dst_ref=lout.at[k],
            send_sem=sem_as.at[k], recv_sem=sem_ar.at[k],
            device_id={"head": k}, device_id_type=MESH,
        )

    pl.semaphore_wait(barrier, 7)

    def compute(b):
        rows = pl.ds(pl.multiple_of(b * Q, Q), Q)
        got = dot(cc_ref[rows, :], inc_ref[...])
        gated = ylg_ref[rows, :].astype(F32) + eg_ref[rows, :].astype(F32) * got
        scale = lax.rsqrt(jnp.mean(gated * gated, axis=1, keepdims=True) + EPSILON)
        normed = (gated * scale * gain_ref[...].astype(F32)).astype(BF16)
        for d in dests:
            @pl.when(b == 0)
            def _():
                w_copy(d, 1 - core).wait()
            psend[b, d] = dot(normed, wv[d * 2 + 1 - core]).astype(BF16)
            pair_copy(b, d).start()

            @pl.when(b == 0)
            def _():
                w_copy(d, core).wait()
            own[b, d] = dot(normed, wv[d * 2 + core])
        low = dot_dims(down_ref[slot_ref[b]], normed, 1, 1).astype(BF16)
        lsend[b] = low

        @pl.when(b == head)
        def _():
            lrecv[b] = low

        @pl.when(b != head)
        def _():
            low_copy(b).start()

    def ring(b, j):
        if j == 0:
            pair_copy(b, dests[0]).wait_recv()
            pair_copy(b, dests[1]).wait_recv()
        elif j == 1:
            pair_copy(b, dests[2]).wait_recv()
        elif j == 3:
            pair_copy(b, dests[3]).wait_recv()
        for way in range(2):
            d = (y + (j + 1) * (3 - 2 * way)) % 4
            part = slice(way * half, way * half + half)
            value = own[b, d, part, :] + precv[b, d, part, :].astype(F32)
            if j > 0:
                ring_copy(b, j - 1, way).wait_recv()
                value = value + rrecv[b, j - 1, way].astype(F32)
            if j < 3:
                rsend[b, j, way] = value.astype(BF16)
                ring_copy(b, j, way).start()
            else:
                at = pl.multiple_of(b * Q + way * half, half)
                base_ref[pl.ds(at, half), :] = value

    def sum_low():
        for k in range(8):
            @pl.when(k != head)
            def _():
                low_arrival(k).wait_recv()
        total = lrecv[0].astype(F32)
        for k in range(1, 8):
            total = total + lrecv[k].astype(F32)
        lout[head] = total.astype(BF16)
        for k in range(8):
            @pl.when(k != head)
            def _():
                sum_copy(k).start()

    def tick(t, carry):
        @pl.when(t < blocks)
        def _():
            compute(t)

        for j in range(4):
            b = t - LAG[j]

            @pl.when(jnp.logical_and(b >= 0, b < blocks))
            def _():
                ring(b, j)

        @pl.when(t == blocks + 1)
        def _():
            sum_low()

        return carry

    lax.fori_loop(0, blocks + LAG[3], tick, 0)

    for k in range(8):
        @pl.when(k != head)
        def _():
            sum_arrival(k).wait_recv()
            low_copy(k).wait_send()
            sum_copy(k).wait_send()
    low_ref[...] = lout[...]

    def drain(b, carry):
        for d in range(4):
            pair_copy(b, d).wait_send()
        for j in range(3):
            for way in range(2):
                ring_copy(b, j, way).wait_send()
        return carry

    lax.fori_loop(0, blocks, drain, 0)


def project(slots, ylg, eg, cc, inc, gain, down, weight):
    tokens, width = ylg.shape
    feat = weight.shape[1] // 8
    rank = down.shape[1]
    blocks = tokens // Q
    vmem = pl.BlockSpec(memory_space=pltpu.VMEM)
    dma = pltpu.SemaphoreType.DMA
    return pl.pallas_call(
        project_kernel,
        in_specs=[pl.BlockSpec(memory_space=pltpu.SMEM)] + [vmem] * 6 + [pl.BlockSpec(memory_space=pl.ANY)],
        out_specs=[vmem, vmem],
        out_shape=[
            jax.ShapeDtypeStruct((tokens, feat), F32),
            jax.ShapeDtypeStruct((blocks, rank, Q), BF16),
        ],
        scratch_shapes=[
            pltpu.VMEM((8, width, feat), BF16),
            pltpu.VMEM((blocks, 4, Q, feat), F32),
            pltpu.VMEM((blocks, 4, Q, feat), BF16),
            pltpu.VMEM((blocks, 4, Q, feat), BF16),
            pltpu.VMEM((blocks, 3, 2, Q // 2, feat), BF16),
            pltpu.VMEM((blocks, 3, 2, Q // 2, feat), BF16),
            pltpu.VMEM((8, rank, Q), BF16),
            pltpu.VMEM((8, rank, Q), BF16),
            pltpu.VMEM((8, rank, Q), BF16),
            dma((8,)), dma((blocks, 4)), dma((blocks, 4)), dma((blocks, 3, 2)), dma((blocks, 3, 2)),
            dma((8,)), dma((8,)), dma((8,)), dma((8,)),
        ],
        compiler_params=pltpu.CompilerParams(
            collective_id=2, has_side_effects=True, vmem_limit_bytes=VMEM_LIMIT
        ),
        name="project",
    )(slots, ylg, eg, cc, inc, gain, down, weight)


def adapt_kernel(slot_ref, base_ref, low_ref, up_ref, out_ref):
    out_ref[...] = (base_ref[...] + dot_dims(low_ref[0], up_ref[0], 0, 0)).astype(BF16)


def adapt(slots, base, low, up):
    tokens, feat = base.shape
    rank = low.shape[1]
    return pl.pallas_call(
        adapt_kernel,
        grid_spec=pltpu.PrefetchScalarGridSpec(
            num_scalar_prefetch=1,
            grid=(tokens // Q,),
            in_specs=[
                pl.BlockSpec((Q, feat), lambda i, s: (i, 0)),
                pl.BlockSpec((1, rank, Q), lambda i, s: (i, 0, 0)),
                pl.BlockSpec((1, rank, feat), lambda i, s: (s[i], 0, 0)),
            ],
            out_specs=pl.BlockSpec((Q, feat), lambda i, s: (i, 0)),
        ),
        out_shape=jax.ShapeDtypeStruct((tokens, feat), BF16),
        compiler_params=pltpu.CompilerParams(vmem_limit_bytes=16 * 1024 * 1024),
        name="adapt",
    )(slots, base, low, up)


def local(
    input_x_channels,
    input_b_channels,
    input_c_channels,
    input_gate_channels,
    raw_step_sizes,
    log_decay_rate,
    head_skip_coeff,
    x_conv_taps,
    b_conv_taps,
    c_conv_taps,
    gated_norm_gain,
    output_weight,
    adapter_down_panels,
    adapter_up_panels,
    turn_first_token,
    tenant_of_turn,
    tenant_panel_index,
):
    tokens = input_x_channels.shape[0]
    own = lax.axis_index("ctx")
    slot_turns = jnp.maximum(TURN_DEV * own - 1 + jnp.arange(TURN_DEV + 1), 0)
    homes = jnp.take(tenant_panel_index, jnp.take(tenant_of_turn, slot_turns))
    starts = lax.dynamic_slice_in_dim(turn_first_token, TURN_DEV * own, TURN_DEV, 0)
    places = own * tokens + Q * jnp.arange(tokens // Q)
    slots = jnp.sum((places[:, None] >= starts[None, :]).astype(jnp.int32), axis=1)

    all_down = lax.all_gather(adapter_down_panels.transpose(0, 2, 1), "ctx", axis=0, tiled=True)
    all_up = lax.all_gather(adapter_up_panels, "ctx", axis=0, tiled=True)
    down = jnp.take(all_down, homes, axis=0)
    up = jnp.take(all_up, homes, axis=0)

    tails = jnp.concatenate(
        [input_x_channels[tokens - 8 :], input_b_channels[tokens - 8 :], input_c_channels[tokens - 8 :]],
        axis=1,
    )
    count = lax.axis_size("ctx")
    halo = lax.ppermute(tails, "ctx", [(i, i + 1) for i in range(count - 1)])
    ylg, eg, cc, state, decay = local_scan(
        input_x_channels, input_b_channels, input_c_channels, input_gate_channels, raw_step_sizes,
        log_decay_rate, head_skip_coeff, halo, x_conv_taps, b_conv_taps, c_conv_taps,
    )
    inc = exchange(state, decay)
    base, low = project(slots, ylg, eg, cc, inc, gated_norm_gain.reshape(1, -1), down, output_weight)
    return adapt(slots, base, low, up)


def solution(mesh):
    in_specs = (
        P("ctx", "head"),
        P("ctx", "head"),
        P("ctx", "head"),
        P("ctx", "head"),
        P("head", "ctx"),
        P("head"),
        P("head"),
        P(None, "head"),
        P(None, "head"),
        P(None, "head"),
        P("head"),
        P("head", None),
        P("ctx", "head", None),
        P("ctx", None, "head"),
        P(),
        P(),
        P(),
    )
    out_specs = P("ctx", "head")
    return jax.shard_map(local, mesh=mesh, in_specs=in_specs, out_specs=out_specs, check_vma=False)
```

time: 351 us -> 249 us (0.71)
  Pallas kernels: 0 us -> 124 us
  blocking collectives: 67.5 us -> 0 us
  matrix products: 52.3 us -> 0 us
  waiting for transfers between devices: 135 us -> 87.9 us
  other arithmetic: 36.4 us -> 1.66 us
  local copies, waits for them, and re-layouts: 32.7 us -> 17.6 us
  starting transfers between devices: 11.4 us -> 3.93 us
    pallas_call x0 -> x4, Pallas kernels: none -> 124 us  [the longest x1 57.3 us: project(): pl.pallas_call(project_kernel, in_specs=[pl.BlockSpec(memory_space=pltpu....]
    dot_general x9 -> x0, matrix products: 49.5 us -> none  [the longest x1 12.8 us: local(): incoming = jnp.einsum('jgh,jghpn->ghpn', weights, states, precision=highest)]
    unnamed x1 -> x0, blocking collectives: 36.2 us -> none
    psum x1 -> x0, blocking collectives: 31.3 us -> none  [local(): rank_reduced = lax.psum(rank_reduced, 'head').astype(jnp.bfloat16)]
    all_gather x3 -> x2, waiting for transfers between devices: 117 us -> 86.5 us  [the longest x1 86.5 us: local(): lax.all_gather(adapter_down_panels.transpose(0, 2, 1), 'ctx', axis=0, til...]
    reduce_scatter x1 -> x0, waiting for transfers between devices: 16.4 us -> none  [local(): lax.psum_scatter(jnp.dot(y_normed, output_weight, preferred_element_type=...]
    unnamed x44 -> x10, local copies, waits for them, and re-layouts: 15.9 us -> 3.09 us
    add x9 -> x1, other arithmetic: 9.3 us -> 0.01 us  [local(): places = own * tokens + Q * jnp.arange(tokens // Q)]
  transfers between devices with their start and end apart: 7 -> 3, of which waited for: 4 -> 1; matrix products, arithmetic and copies ran while one was open for 24% -> 4% of each run, Pallas kernels for 0% -> 25%
where the time goes in v1:
time: 249 us
  Pallas kernels  124 us (50%)
  waiting for transfers between devices  87.9 us (35%)
  local copies, waits for them, and re-layouts  17.6 us (7%)
  between operations  13.5 us (5%)
  starting transfers between devices  3.93 us (2%)
    all_gather x1, waiting for transfers between devices, local(): lax.all_gather(adapter_down_panels.transpose(0, 2, 1), 'ctx', axis=0, til...  86.5 us
    pallas_call x1, Pallas kernels, project(): pl.pallas_call(project_kernel, in_specs=[pl.BlockSpec(memory_space=pltpu....  57.3 us
    pallas_call x1, Pallas kernels, exchange(): pl.pallas_call(functools.partial(exchange_kernel, chunks=chunks), in_spec...  42.4 us
    pallas_call x1, Pallas kernels, local_scan(): pl.pallas_call(scan_kernel, grid=(tokens // Q,), in_specs=[smem, smem, ro...  20 us
    gather x1, local copies, waits for them, and re-layouts, local(): down = jnp.take(all_down, homes, axis=0)  5.15 us
  transfers between devices with their start and end apart: 3, of which 1 were waited for; matrix products, arithmetic and copies ran while one was open for 4% of the time, Pallas kernels for 25%

profile of v1, /device:TPU:0, one launch (start us, length us, event | category | flops | bytes accessed | tf_op | source)
XLA Modules:
  0.0 248.6 jit_solution(11536977735892125645)
XLA Ops:
  6.5 0.0 copy-start
  6.5 0.0 all-gather.5.cloned.1.call-start
  6.5 0.7 all-gather.5.cloned.1.call-update
  7.3 0.0 all-gather.3.cloned.1.call-start
  7.3 0.7 all-gather.3.cloned.1.call-update
  8.0 0.7 slice.9
  8.7 0.7 slice.10
  9.4 0.7 slice.11
  10.1 3.9 %collective-permute-start = (bf16[8,1280]{1,0:T(8,128)(2,1)S(1)}, bf16[8,1280]{1,0:T(8,128)(2,1)S(1)}, u32[]{:S(2)}, u32[]{:S(2)}) collective-permute-start(bf16[8,1280]{1,0:T(8,128)(2,1)S(1)} %pad_maximum_fusion), channel_id=1, source_target_pairs={{0,8},{8,16},{16,24},{24,32},{32,40},{40,48},{48,56},{56,64},{64,7... | collective-permute-start | bytes 61448 | tf_op jit(solution)/shard_map/ppermute | solution.py:561
  14.0 0.0 copy-done
  14.0 0.6 gather_fusion
  14.7 1.3 gather_fusion.1
  16.0 0.7 dynamic_slice.3
  16.7 0.7 fusion.slot_ref
  17.4 1.3 reshape.87.gain_ref
  18.7 0.0 collective-permute-done.halo_ref
  18.7 0.0 copy-start.4
  18.7 0.6 copy-done.4
  19.3 20.0 %local_scan.1 = (bf16[1024,1024]{1,0:T(8,128)(2,1)}, bf16[1024,1024]{1,0:T(8,128)(2,1)}, bf16[1024,128]{1,0:T(8,128)(2,1)}, f32[128,1024]{1,0:T(8,128)}, f32[8,1024]{1,0:T(8,128)}) custom-call(f32[16]{0:T(128)} %rate_ref.1, f32[16]{0:T(128)} %skip_ref.1, bf16[1024,1024]{1,0:T(8,128)(2,1)} %x_ref.1, bf16[1024,128]{1,0:T(8,128)(2,1)} %b_ref.1, ...), custom_call_target="tpu_custom_call" | custom-call | tf_op jit(solution)/shard_map/local_scan/pallas_call | solution.py:139
  39.4 42.4 %state_exchange.1.inc_ref = bf16[128,1024]{1,0:T(8,128)(2,1)} custom-call(f32[128,1024]{1,0:T(8,128)} %get-tuple-element.15.s_ref, f32[8,1024]{1,0:T(8,128)} %get-tuple-element.16.d_ref), custom_call_target="tpu_custom_call" | custom-call | tf_op jit(solution)/shard_map/state_exchange/pallas_call | solution.py:260
  81.7 0.0 all-gather.5.cloned.1.call-done
  81.8 3.3 %gather_fusion.3 = bf16[3,64,512]{2,1,0:T(8,128)(2,1)S(1)} fusion(bf16[96,64,512]{2,1,0:T(8,128)(2,1)} %all-gather.5.cloned.1.call-done, s32[1024]{0:T(1024)S(1)} %pad_clamp_fusion), kind=kCustom, calls=%fused_computation.3 | custom fusion | bytes 393228 | tf_op jit(solution)/shard_map/jit(_take)/gather | solution.py:554
  85.1 0.1 broadcast_select_fusion.1.up_ref
  85.2 86.5 %all-gather.3.cloned.1.call-done = bf16[96,64,1024]{2,1,0:T(8,128)(2,1)} async-done(((bf16[6,64,1024]{2,1,0:T(8,128)(2,1)}), bf16[96,64,1024]{2,1,0:T(8,128)(2,1)}) %all-gather.3.cloned.1.call-update) | async-done | bytes 12582928 | tf_op jit(solution)/shard_map/all_gather | solution.py:551
  171.7 5.1 %gather_fusion.2 = bf16[3,64,1024]{2,1,0:T(8,128)(2,1)S(1)} fusion(bf16[96,64,1024]{2,1,0:T(8,128)(2,1)} %all-gather.3.cloned.1.call-done, s32[1024]{0:T(1024)S(1)} %pad_clamp_fusion), kind=kCustom, calls=%fused_computation.2 | custom fusion | bytes 786444 | tf_op jit(solution)/shard_map/jit(_take)/gather | solution.py:553
  176.9 0.8 broadcast_select_fusion.down_ref
  177.7 57.3 %project.1 = (f32[1024,512]{1,0:T(8,128)}, bf16[8,64,128]{2,1,0:T(8,128)(2,1)}) custom-call(s32[8]{0:T(128)} %fusion.slot_ref, bf16[1024,1024]{1,0:T(8,128)(2,1)} %get-tuple-element.12.ylg_ref, bf16[1024,1024]{1,0:T(8,128)(2,1)} %get-tuple-element.13.eg_ref, bf16[1024,128]{1,0:T(8,128)(2,1)} %get-tuple-element.14.cc_ref, ...), custom_call_target="tpu_custom_call" | custom-call | tf_op jit(solution)/shard_map/project/pallas_call | solution.py:471
  235.0 0.0 copy-done.3
  235.0 0.0 copy-start.1
  235.0 1.6 copy-done.1
  236.6 0.9 copy-done.2
  237.5 4.3 %adapt.1 = bf16[1024,512]{1,0:T(8,128)(2,1)} custom-call(s32[8]{0:T(128)S(1)} %copy-done.3, f32[1024,512]{1,0:T(8,128)S(1)} %copy-done.1, bf16[8,64,128]{2,1,0:T(8,128)(2,1)S(1)} %copy-done.2, bf16[3,64,512]{2,1,0:T(8,128)(2,1)S(1)} %broadcast_select_fusion.1.up_ref), custom_call_target="tpu_custom_call" | custom-call | tf_op jit(solution)/shard_map/adapt/pallas_call | solution.py:506
  (11 shorter events, 0.1 us)
Async XLA Ops:
  6.5 7.5 %copy-start = (s32[32]{0:T(128)S(1)}, s32[32]{0:T(128)}, u32[]{:S(2)}) copy-start(s32[32]{0:T(128)} %param.32) | copy-start | bytes 388
  6.5 75.2 %all-gather.5.cloned.1.call-start = ((), (), s32[]{:S(2)}) async-start(), calls=%async_computation.1 | async-start | bytes 6684672 | tf_op jit(solution)/shard_map/all_gather | solution.py:552
  7.3 164.5 %all-gather.3.cloned.1.call-start = ((), (), s32[]{:S(2)}) async-start(), calls=%async_computation | async-start | bytes 13369344 | tf_op jit(solution)/shard_map/all_gather | solution.py:551
  10.1 8.6 %collective-permute-start = (bf16[8,1280]{1,0:T(8,128)(2,1)S(1)}, bf16[8,1280]{1,0:T(8,128)(2,1)S(1)}, u32[]{:S(2)}, u32[]{:S(2)}) collective-permute-start(bf16[8,1280]{1,0:T(8,128)(2,1)S(1)} %pad_maximum_fusion), channel_id=1, source_target_pairs={{0,8},{8,16},{16,24},{24,32},{32,40},{40,48},{48,56},{56,64},{64,7... | collective-permute-start | bytes 61448 | tf_op jit(solution)/shard_map/ppermute | solution.py:561
  18.7 0.6 copy-start.4
  177.7 57.3 %copy-start.3 = (s32[8]{0:T(128)S(1)}, s32[8]{0:T(128)}, u32[]{:S(2)}) copy-start(s32[8]{0:T(128)} %fusion.slot_ref) | copy-start | bytes 100
  235.0 1.6 copy-start.1
  236.6 0.9 copy-start.2
Sparse Core Ops, SparseCore 0:
  9.5 70.2 all-gather.4
  82.1 89.6 all-gather.2

commit v2 on v1

--- a/solution.py
+++ b/solution.py
@@ -11,6 +11,7 @@
 N = 128
 Q = 128
 TURN_DEV = 2
+PANEL_DEV = 6
 LOG2E = 1.4426950408889634
 EPSILON = 1e-05
 VMEM_LIMIT = 60 * 1024 * 1024
@@ -375,7 +376,7 @@
             def _():
                 w_copy(d, core).wait()
             own[b, d] = dot(normed, wv[d * 2 + core])
-        low = dot_dims(down_ref[slot_ref[b]], normed, 1, 1).astype(BF16)
+        low = dot_dims(down_ref[slot_ref[b], :, 0 : ylg_ref.shape[1]], normed, 1, 1).astype(BF16)
         lsend[b] = low
 
         @pl.when(b == head)
@@ -496,6 +497,36 @@
     )(slots, ylg, eg, cc, inc, gain, down, weight)
 
 
+def lay_out_kernel(place_ref, down_ref, up_ref, out_ref):
+    group, width = out_ref.shape[0], down_ref.shape[2]
+    for k in range(group):
+        place = place_ref[pl.program_id(0) * group + k]
+        here = jnp.logical_and(place >= 0, place < PANEL_DEV)
+        index = jnp.clip(place, 0, PANEL_DEV - 1)
+        out_ref[k, :, 0:width] = jnp.where(here, down_ref[index], 0)
+        out_ref[k, :, width:] = jnp.where(here, up_ref[index], 0)
+
+
+def lay_out(places, down, up, group=4):
+    turns = places.shape[0]
+    rank, width = down.shape[1:]
+    total = width + up.shape[2]
+    return pl.pallas_call(
+        lay_out_kernel,
+        grid_spec=pltpu.PrefetchScalarGridSpec(
+            num_scalar_prefetch=1,
+            grid=(turns // group,),
+            in_specs=[
+                pl.BlockSpec(down.shape, lambda i, s: (0, 0, 0)),
+                pl.BlockSpec(up.shape, lambda i, s: (0, 0, 0)),
+            ],
+            out_specs=pl.BlockSpec((group, rank, total), lambda i, s: (i, 0, 0)),
+        ),
+        out_shape=jax.ShapeDtypeStruct((turns, rank, total), BF16),
+        name="lay_out",
+    )(places, down, up)
+
+
 def adapt_kernel(slot_ref, base_ref, low_ref, up_ref, out_ref):
     out_ref[...] = (base_ref[...] + dot_dims(low_ref[0], up_ref[0], 0, 0)).astype(BF16)
 
@@ -511,7 +542,7 @@
             in_specs=[
                 pl.BlockSpec((Q, feat), lambda i, s: (i, 0)),
                 pl.BlockSpec((1, rank, Q), lambda i, s: (i, 0, 0)),
-                pl.BlockSpec((1, rank, feat), lambda i, s: (s[i], 0, 0)),
+                pl.BlockSpec((1, rank, feat), lambda i, s: (s[i], 0, up.shape[2] // feat - 1)),
             ],
             out_specs=pl.BlockSpec((Q, feat), lambda i, s: (i, 0)),
         ),
@@ -542,30 +573,30 @@
 ):
     tokens = input_x_channels.shape[0]
     own = lax.axis_index("ctx")
-    slot_turns = jnp.maximum(TURN_DEV * own - 1 + jnp.arange(TURN_DEV + 1), 0)
-    homes = jnp.take(tenant_panel_index, jnp.take(tenant_of_turn, slot_turns))
+    homes = jnp.take(tenant_panel_index, tenant_of_turn)
     starts = lax.dynamic_slice_in_dim(turn_first_token, TURN_DEV * own, TURN_DEV, 0)
     places = own * tokens + Q * jnp.arange(tokens // Q)
     slots = jnp.sum((places[:, None] >= starts[None, :]).astype(jnp.int32), axis=1)
 
-    all_down = lax.all_gather(adapter_down_panels.transpose(0, 2, 1), "ctx", axis=0, tiled=True)
-    all_up = lax.all_gather(adapter_up_panels, "ctx", axis=0, tiled=True)
-    down = jnp.take(all_down, homes, axis=0)
-    up = jnp.take(all_up, homes, axis=0)
+    offered = lay_out(homes - PANEL_DEV * own, adapter_down_panels.transpose(0, 2, 1), adapter_up_panels)
+    count = lax.axis_size("ctx")
+    onward = [(i, i + 1) for i in range(count - 1)]
+    mine = lax.psum_scatter(offered, "ctx", scatter_dimension=0, tiled=True)
+    before = lax.ppermute(mine[TURN_DEV - 1 :], "ctx", onward)
+    panels = jnp.concatenate([before, mine], axis=0)
 
     tails = jnp.concatenate(
         [input_x_channels[tokens - 8 :], input_b_channels[tokens - 8 :], input_c_channels[tokens - 8 :]],
         axis=1,
     )
-    count = lax.axis_size("ctx")
-    halo = lax.ppermute(tails, "ctx", [(i, i + 1) for i in range(count - 1)])
+    halo = lax.ppermute(tails, "ctx", onward)
     ylg, eg, cc, state, decay = local_scan(
         input_x_channels, input_b_channels, input_c_channels, input_gate_channels, raw_step_sizes,
         log_decay_rate, head_skip_coeff, halo, x_conv_taps, b_conv_taps, c_conv_taps,
     )
     inc = exchange(state, decay)
-    base, low = project(slots, ylg, eg, cc, inc, gated_norm_gain.reshape(1, -1), down, output_weight)
-    return adapt(slots, base, low, up)
+    base, low = project(slots, ylg, eg, cc, inc, gated_norm_gain.reshape(1, -1), panels, output_weight)
+    return adapt(slots, base, low, panels)
 
 
 def solution(mesh):

time: 249 us -> 234 us (0.940)
  local copies, waits for them, and re-layouts: 17.6 us -> 8.02 us
  waiting for transfers between devices: 87.9 us -> 79.4 us
  starting transfers between devices: 3.93 us -> 6.98 us
    all_gather x2 -> x0, waiting for transfers between devices: 86.5 us -> none  [the longest x1 86.5 us: local(): lax.all_gather(adapter_down_panels.transpose(0, 2, 1), 'ctx', axis=0, til...]
    reduce_scatter x0 -> x1, waiting for transfers between devices: none -> 79.4 us  [local(): mine = lax.psum_scatter(offered, 'ctx', scatter_dimension=0, tiled=True)]
    gather x4 -> x1, local copies, waits for them, and re-layouts: 10.4 us -> 0.7 us  [local(): homes = jnp.take(tenant_panel_index, tenant_of_turn)]
    pallas_call x1, Pallas kernels: 42.4 us -> 35.6 us  [exchange(): pl.pallas_call(functools.partial(exchange_kernel, chunks=chunks), in_spec...]
    pallas_call x0 -> x1, Pallas kernels: none -> 6.2 us  [lay_out(): pl.pallas_call(lay_out_kernel, grid_spec=pltpu.PrefetchScalarGridSpec(num...]
    ppermute x1 -> x2, starting transfers between devices: 3.89 us -> 6.98 us  [the longest x1 3.91 us: local(): halo = lax.ppermute(tails, 'ctx', onward)]
    unnamed x10 -> x21, local copies, waits for them, and re-layouts: 3.09 us -> 5 us
  transfers between devices with their start and end apart: 3 -> 3, of which waited for: 1 -> 1; matrix products, arithmetic and copies ran while one was open for 4% -> 1% of each run, Pallas kernels for 25% -> 24%
where the time goes in v2:
time: 234 us
  Pallas kernels  123 us (53%)
  waiting for transfers between devices  79.4 us (34%)
  between operations  13.5 us (6%)
  local copies, waits for them, and re-layouts  8.02 us (3%)
  starting transfers between devices  6.98 us (3%)
  other arithmetic  2.49 us (1%)
    reduce_scatter x1, waiting for transfers between devices, local(): mine = lax.psum_scatter(offered, 'ctx', scatter_dimension=0, tiled=True)  79.4 us
    pallas_call x1, Pallas kernels, project(): pl.pallas_call(project_kernel, in_specs=[pl.BlockSpec(memory_space=pltpu....  57.2 us
    pallas_call x1, Pallas kernels, exchange(): pl.pallas_call(functools.partial(exchange_kernel, chunks=chunks), in_spec...  35.6 us
    pallas_call x1, Pallas kernels, local_scan(): pl.pallas_call(scan_kernel, grid=(tokens // Q,), in_specs=[smem, smem, ro...  20 us
    pallas_call x1, Pallas kernels, lay_out(): pl.pallas_call(lay_out_kernel, grid_spec=pltpu.PrefetchScalarGridSpec(num...  6.2 us
    unnamed x21, local copies, waits for them, and re-layouts  5 us
  transfers between devices with their start and end apart: 3, of which 1 were waited for; matrix products, arithmetic and copies ran while one was open for 1% of the time, Pallas kernels for 24%

profile of v2, /device:TPU:0, one launch (start us, length us, event | category | flops | bytes accessed | tf_op | source)
XLA Modules:
  0.0 233.9 jit_solution(12802667218769357954)
XLA Ops:
  6.5 0.0 copy-start
  6.5 0.0 reduce-scatter.2.cloned.1.call-start
  6.5 0.7 compare_select_fusion
  7.2 0.0 copy-done
  7.2 0.7 gather_fusion
  7.9 1.2 fusion.1.place_ref
  9.1 6.2 %lay_out.1 = bf16[32,64,1536]{2,1,0:T(8,128)(2,1)} custom-call(s32[32]{0:T(128)} %fusion.1.place_ref, bf16[6,64,1024]{2,1,0:T(8,128)(2,1)} %bitcast.1, bf16[6,64,512]{2,1,0:T(8,128)(2,1)} %up_ref.1), custom_call_target="tpu_custom_call" | custom-call | tf_op jit(solution)/shard_map/lay_out/pallas_call | solution.py:514
  15.3 0.0 copy-start.8
  15.3 0.0 reduce-scatter.2.cloned.1.call-update
  15.3 0.7 slice-done
  16.0 0.0 slice-done.1
  16.0 0.0 slice-done.2
  16.0 3.9 %collective-permute-start = (bf16[8,1280]{1,0:T(8,128)(2,1)S(1)}, bf16[8,1280]{1,0:T(8,128)(2,1)S(1)}, u32[]{:S(2)}, u32[]{:S(2)}) collective-permute-start(bf16[8,1280]{1,0:T(8,128)(2,1)S(1)} %pad_maximum_fusion), channel_id=1, source_target_pairs={{0,8},{8,16},{16,24},{24,32},{32,40},{40,48},{48,56},{56,64},{64,7... | collective-permute-start | bytes 61448 | tf_op jit(solution)/shard_map/ppermute | solution.py:592
  20.0 0.1 dynamic_slice.3
  20.0 79.4 %reduce-scatter.2.cloned.1.call-done = bf16[2,64,1536]{2,1,0:T(8,128)(2,1)} async-done(((bf16[32,64,1536]{2,1,0:T(8,128)(2,1)}), bf16[2,64,1536]{2,1,0:T(8,128)(2,1)}) %reduce-scatter.2.cloned.1.call-update) | async-done | bytes 393232 | tf_op jit(solution)/shard_map/reduce_scatter | solution.py:584
  99.4 0.9 slice.18
  100.4 3.1 %collective-permute-start.1 = (bf16[1,64,1536]{2,1,0:T(8,128)(2,1)S(1)}, bf16[1,64,1536]{2,1,0:T(8,128)(2,1)S(1)}, u32[]{:S(2)}, u32[]{:S(2)}) collective-permute-start(bf16[1,64,1536]{2,1,0:T(8,128)(2,1)S(1)} %slice.18), channel_id=1, source_target_pairs={{0,8},{8,16},{16,24},{24,32},{32,40},{40,48},{48,56},{56,64},{64,7... | collective-permute-start | bytes 589832 | tf_op jit(solution)/shard_map/ppermute | solution.py:585
  103.5 0.6 fusion.slot_ref
  104.1 0.6 reshape.14.gain_ref
  104.7 0.0 collective-permute-done.halo_ref
  104.7 0.6 copy-done.7
  105.3 20.0 %local_scan.1 = (bf16[1024,1024]{1,0:T(8,128)(2,1)}, bf16[1024,1024]{1,0:T(8,128)(2,1)}, bf16[1024,128]{1,0:T(8,128)(2,1)}, f32[128,1024]{1,0:T(8,128)}, f32[8,1024]{1,0:T(8,128)}) custom-call(f32[16]{0:T(128)} %rate_ref.1, f32[16]{0:T(128)} %skip_ref.1, bf16[1024,1024]{1,0:T(8,128)(2,1)} %x_ref.1, bf16[1024,128]{1,0:T(8,128)(2,1)} %b_ref.1, ...), custom_call_target="tpu_custom_call" | custom-call | tf_op jit(solution)/shard_map/local_scan/pallas_call | solution.py:140
  125.4 35.6 %state_exchange.1.inc_ref = bf16[128,1024]{1,0:T(8,128)(2,1)} custom-call(f32[128,1024]{1,0:T(8,128)} %get-tuple-element.15.s_ref, f32[8,1024]{1,0:T(8,128)} %get-tuple-element.16.d_ref), custom_call_target="tpu_custom_call" | custom-call | tf_op jit(solution)/shard_map/state_exchange/pallas_call | solution.py:261
  161.0 0.0 collective-permute-done.1
  161.1 0.0 copy-start.1
  161.1 0.8 copy-done.1
  161.9 57.2 %project.1 = (f32[1024,512]{1,0:T(8,128)}, bf16[8,64,128]{2,1,0:T(8,128)(2,1)}) custom-call(s32[8]{0:T(128)} %fusion.slot_ref, bf16[1024,1024]{1,0:T(8,128)(2,1)} %get-tuple-element.12.ylg_ref, bf16[1024,1024]{1,0:T(8,128)(2,1)} %get-tuple-element.13.eg_ref, bf16[1024,128]{1,0:T(8,128)(2,1)} %get-tuple-element.14.cc_ref, ...), custom_call_target="tpu_custom_call" | custom-call | tf_op jit(solution)/shard_map/project/pallas_call | solution.py:472
  219.1 0.0 copy-start.2
  219.2 1.1 copy-done.2
  220.2 1.6 copy-done.3
  221.8 0.9 copy-done.4
  222.7 4.3 %adapt.1 = bf16[1024,512]{1,0:T(8,128)(2,1)} custom-call(s32[8]{0:T(128)S(1)} %copy-done.5, f32[1024,512]{1,0:T(8,128)S(1)} %copy-done.3, bf16[8,64,128]{2,1,0:T(8,128)(2,1)S(1)} %copy-done.4, bf16[3,64,1536]{2,1,0:T(8,128)(2,1)S(1)} %copy-done.2), custom_call_target="tpu_custom_call" | custom-call | tf_op jit(solution)/shard_map/adapt/pallas_call | solution.py:537
  (18 shorter events, 0.1 us)
Async XLA Ops:
  6.5 0.7 copy-start
  6.5 92.9 %reduce-scatter.2.cloned.1.call-start = ((), (), s32[]{:S(2)}) async-start(), calls=%async_computation.1 | async-start | bytes 6684672 | tf_op jit(solution)/shard_map/reduce_scatter | solution.py:584
  15.3 0.7 slice-start
  15.3 0.7 slice-start.1
  15.3 0.7 slice-start.2
  15.3 4.6 %copy-start.9 = (s32[32]{0:T(128)S(1)}, s32[32]{0:T(128)}, u32[]{:S(2)}) copy-start(s32[32]{0:T(128)} %param.31) | copy-start | bytes 388
  15.3 88.8 %copy-start.8 = (bf16[1024]{0:T(1024)(128)(2,1)S(1)}, bf16[1024]{0:T(1024)(128)(2,1)}, u32[]{:S(2)}) copy-start(bf16[1024]{0:T(1024)(128)(2,1)} %param.27) | copy-start | bytes 6148
  16.0 88.7 %collective-permute-start = (bf16[8,1280]{1,0:T(8,128)(2,1)S(1)}, bf16[8,1280]{1,0:T(8,128)(2,1)S(1)}, u32[]{:S(2)}, u32[]{:S(2)}) collective-permute-start(bf16[8,1280]{1,0:T(8,128)(2,1)S(1)} %pad_maximum_fusion), channel_id=1, source_target_pairs={{0,8},{8,16},{16,24},{24,32},{32,40},{40,48},{48,56},{56,64},{64,7... | collective-permute-start | bytes 61448 | tf_op jit(solution)/shard_map/ppermute | solution.py:592
  100.4 60.6 %collective-permute-start.1 = (bf16[1,64,1536]{2,1,0:T(8,128)(2,1)S(1)}, bf16[1,64,1536]{2,1,0:T(8,128)(2,1)S(1)}, u32[]{:S(2)}, u32[]{:S(2)}) collective-permute-start(bf16[1,64,1536]{2,1,0:T(8,128)(2,1)S(1)} %slice.18), channel_id=1, source_target_pairs={{0,8},{8,16},{16,24},{24,32},{32,40},{40,48},{48,56},{56,64},{64,7... | collective-permute-start | bytes 589832 | tf_op jit(solution)/shard_map/ppermute | solution.py:585
  104.7 56.3 %copy-start.6 = (bf16[2,64,1536]{2,1,0:T(8,128)(2,1)S(1)}, bf16[2,64,1536]{2,1,0:T(8,128)(2,1)}, u32[]{:S(2)}) copy-start(bf16[2,64,1536]{2,1,0:T(8,128)(2,1)} %reduce-scatter.2.cloned.1.call-done) | copy-start | bytes 1179652
  104.7 0.6 copy-start.7
  161.1 0.8 copy-start.1
  161.9 57.2 %copy-start.5 = (s32[8]{0:T(128)S(1)}, s32[8]{0:T(128)}, u32[]{:S(2)}) copy-start(s32[8]{0:T(128)} %fusion.slot_ref) | copy-start | bytes 100
  219.1 1.1 copy-start.2
  220.2 1.6 copy-start.3
  221.8 0.9 copy-start.4
Sparse Core Ops, SparseCore 0:
  15.5 83.9 reduce-scatter.1

commit v3 on v2

--- a/solution.py
+++ b/solution.py
@@ -582,8 +582,6 @@
     count = lax.axis_size("ctx")
     onward = [(i, i + 1) for i in range(count - 1)]
     mine = lax.psum_scatter(offered, "ctx", scatter_dimension=0, tiled=True)
-    before = lax.ppermute(mine[TURN_DEV - 1 :], "ctx", onward)
-    panels = jnp.concatenate([before, mine], axis=0)
 
     tails = jnp.concatenate(
         [input_x_channels[tokens - 8 :], input_b_channels[tokens - 8 :], input_c_channels[tokens - 8 :]],
@@ -595,6 +593,9 @@
         log_decay_rate, head_skip_coeff, halo, x_conv_taps, b_conv_taps, c_conv_taps,
     )
     inc = exchange(state, decay)
+    mine, inc = lax.optimization_barrier((mine, inc))
+    before = lax.ppermute(mine[TURN_DEV - 1 :], "ctx", onward)
+    panels = jnp.concatenate([before, mine], axis=0)
     base, low = project(slots, ylg, eg, cc, inc, gated_norm_gain.reshape(1, -1), panels, output_weight)
     return adapt(slots, base, low, panels)
 

time: 234 us -> 186 us (0.79); the launches traced: 234 us -> 183 us
  waiting for transfers between devices: 79.4 us -> 22.3 us
  Pallas kernels: 123 us -> 129 us
    reduce_scatter x1, waiting for transfers between devices: 79.4 us -> 19 us  [local(): mine = lax.psum_scatter(offered, 'ctx', scatter_dimension=0, tiled=True)]
    pallas_call x1, Pallas kernels: 35.6 us -> 40.6 us  [exchange(): pl.pallas_call(functools.partial(exchange_kernel, chunks=chunks), in_spec...]
    ppermute x1, waiting for transfers between devices: 0.01 us -> 2.47 us  [local(): before = lax.ppermute(mine[TURN_DEV - 1:], 'ctx', onward)]
    unnamed x21 -> x19, local copies, waits for them, and re-layouts: 5 us -> 5.01 us
  transfers between devices with their start and end apart: 3 -> 3, of which waited for: 1 -> 3; matrix products, arithmetic and copies ran while one was open for 1% -> 1% of each run, Pallas kernels for 24% -> 33%
where the time goes in v3:
time: 186 us; the launch traced here: 183 us
  Pallas kernels  129 us (69%)
  waiting for transfers between devices  22.3 us (12%)
  between operations  13.5 us (7%)
  local copies, waits for them, and re-layouts  9.02 us (5%)
  starting transfers between devices  7.01 us (4%)
  other arithmetic  2.54 us (1%)
    pallas_call x1, Pallas kernels, project(): pl.pallas_call(project_kernel, in_specs=[pl.BlockSpec(memory_space=pltpu....  57.3 us
    pallas_call x1, Pallas kernels, exchange(): pl.pallas_call(functools.partial(exchange_kernel, chunks=chunks), in_spec...  40.6 us
    pallas_call x1, Pallas kernels, local_scan(): pl.pallas_call(scan_kernel, grid=(tokens // Q,), in_specs=[smem, smem, ro...  20 us
    reduce_scatter x1, waiting for transfers between devices, local(): mine = lax.psum_scatter(offered, 'ctx', scatter_dimension=0, tiled=True)  19 us
    pallas_call x1, Pallas kernels, lay_out(): pl.pallas_call(lay_out_kernel, grid_spec=pltpu.PrefetchScalarGridSpec(num...  6.22 us
    unnamed x19, local copies, waits for them, and re-layouts  5.01 us
    pallas_call x1, Pallas kernels, adapt(): pl.pallas_call(adapt_kernel, grid_spec=pltpu.PrefetchScalarGridSpec(num_s...  4.3 us
    ppermute x1, starting transfers between devices, local(): halo = lax.ppermute(tails, 'ctx', onward)  3.91 us
  transfers between devices with their start and end apart: 3, of which 3 were waited for; matrix products, arithmetic and copies ran while one was open for 1% of the time, Pallas kernels for 33%

profile of v3, /device:TPU:0, one launch (start us, length us, event | category | flops | bytes accessed | tf_op | source)
XLA Modules:
  0.0 182.9 jit_solution(2504788399516684432)
XLA Ops:
  6.5 0.0 copy-start
  6.5 0.0 reduce-scatter.2.cloned.1.call-start
  6.5 0.7 compare_select_fusion
  7.2 0.0 copy-done
  7.2 0.7 gather_fusion
  7.9 1.2 fusion.1.place_ref
  9.1 6.2 %lay_out.1 = bf16[32,64,1536]{2,1,0:T(8,128)(2,1)} custom-call(s32[32]{0:T(128)} %fusion.1.place_ref, bf16[6,64,1024]{2,1,0:T(8,128)(2,1)} %bitcast.1, bf16[6,64,512]{2,1,0:T(8,128)(2,1)} %up_ref.1), custom_call_target="tpu_custom_call" | custom-call | tf_op jit(solution)/shard_map/lay_out/pallas_call | solution.py:514
  15.3 0.0 copy-start.8
  15.3 0.0 reduce-scatter.2.cloned.1.call-update
  15.4 0.7 slice-done
  16.0 0.0 slice-done.1
  16.0 3.9 %collective-permute-start = (bf16[8,1280]{1,0:T(8,128)(2,1)S(1)}, bf16[8,1280]{1,0:T(8,128)(2,1)S(1)}, u32[]{:S(2)}, u32[]{:S(2)}) collective-permute-start(bf16[8,1280]{1,0:T(8,128)(2,1)S(1)} %pad_maximum_fusion), channel_id=1, source_target_pairs={{0,8},{8,16},{16,24},{24,32},{32,40},{40,48},{48,56},{56,64},{64,7... | collective-permute-start | bytes 61448 | tf_op jit(solution)/shard_map/ppermute | solution.py:590
  20.0 0.6 reshape.14.gain_ref
  20.6 0.1 dynamic_slice.3
  20.6 0.8 collective-permute-done.halo_ref
  21.4 0.6 copy-done.6
  22.0 20.0 %local_scan.1 = (bf16[1024,1024]{1,0:T(8,128)(2,1)}, bf16[1024,1024]{1,0:T(8,128)(2,1)}, bf16[1024,128]{1,0:T(8,128)(2,1)}, f32[128,1024]{1,0:T(8,128)}, f32[8,1024]{1,0:T(8,128)}) custom-call(f32[16]{0:T(128)} %rate_ref.1, f32[16]{0:T(128)} %skip_ref.1, bf16[1024,1024]{1,0:T(8,128)(2,1)} %x_ref.1, bf16[1024,128]{1,0:T(8,128)(2,1)} %b_ref.1, ...), custom_call_target="tpu_custom_call" | custom-call | tf_op jit(solution)/shard_map/local_scan/pallas_call | solution.py:140
  42.1 40.6 %state_exchange.1.inc_ref = bf16[128,1024]{1,0:T(8,128)(2,1)} custom-call(f32[128,1024]{1,0:T(8,128)} %get-tuple-element.17.s_ref, f32[8,1024]{1,0:T(8,128)} %get-tuple-element.18.d_ref), custom_call_target="tpu_custom_call" | custom-call | tf_op jit(solution)/shard_map/state_exchange/pallas_call | solution.py:261
  82.7 19.0 %reduce-scatter.2.cloned.1.call-done = bf16[2,64,1536]{2,1,0:T(8,128)(2,1)} async-done(((bf16[32,64,1536]{2,1,0:T(8,128)(2,1)}), bf16[2,64,1536]{2,1,0:T(8,128)(2,1)}) %reduce-scatter.2.cloned.1.call-update) | async-done | bytes 393232 | tf_op jit(solution)/shard_map/reduce_scatter | solution.py:584
  101.8 0.9 slice.15
  102.7 3.1 %collective-permute-start.1 = (bf16[1,64,1536]{2,1,0:T(8,128)(2,1)S(1)}, bf16[1,64,1536]{2,1,0:T(8,128)(2,1)S(1)}, u32[]{:S(2)}, u32[]{:S(2)}) collective-permute-start(bf16[1,64,1536]{2,1,0:T(8,128)(2,1)S(1)} %slice.15), channel_id=1, source_target_pairs={{0,8},{8,16},{16,24},{24,32},{32,40},{40,48},{48,56},{56,64},{64,7... | collective-permute-start | bytes 589832 | tf_op jit(solution)/shard_map/ppermute | solution.py:597
  105.8 0.7 fusion.slot_ref
  106.5 2.5 %collective-permute-done.1 = bf16[1,64,1536]{2,1,0:T(8,128)(2,1)S(1)} collective-permute-done((bf16[1,64,1536]{2,1,0:T(8,128)(2,1)S(1)}, bf16[1,64,1536]{2,1,0:T(8,128)(2,1)S(1)}, u32[]{:S(2)}, u32[]{:S(2)}) %collective-permute-start.1) | collective-permute-done | bytes 196640 | tf_op jit(solution)/shard_map/ppermute | solution.py:597
  109.0 1.0 constant_dynamic-update-slice_fusion.down_ref.up_ref
  110.0 0.0 copy-start.1
  110.0 0.8 copy-done.1
  110.8 57.3 %project.1 = (f32[1024,512]{1,0:T(8,128)}, bf16[8,64,128]{2,1,0:T(8,128)(2,1)}) custom-call(s32[8]{0:T(128)} %fusion.slot_ref, bf16[1024,1024]{1,0:T(8,128)(2,1)} %get-tuple-element.14.ylg_ref, bf16[1024,1024]{1,0:T(8,128)(2,1)} %get-tuple-element.15.eg_ref, bf16[1024,128]{1,0:T(8,128)(2,1)} %get-tuple-element.16.cc_ref, ...), custom_call_target="tpu_custom_call" | custom-call | tf_op jit(solution)/shard_map/project/pallas_call | solution.py:472
  168.2 0.0 copy-start.2
  168.2 1.1 copy-done.2
  169.3 1.6 copy-done.3
  170.8 0.9 copy-done.4
  171.8 4.3 %adapt.1 = bf16[1024,512]{1,0:T(8,128)(2,1)} custom-call(s32[8]{0:T(128)S(1)} %copy-done.5, f32[1024,512]{1,0:T(8,128)S(1)} %copy-done.3, bf16[8,64,128]{2,1,0:T(8,128)(2,1)S(1)} %copy-done.4, bf16[3,64,1536]{2,1,0:T(8,128)(2,1)S(1)} %copy-done.2), custom_call_target="tpu_custom_call" | custom-call | tf_op jit(solution)/shard_map/adapt/pallas_call | solution.py:537
  (16 shorter events, 0.1 us)
Async XLA Ops:
  6.5 0.7 copy-start
  6.5 95.2 %reduce-scatter.2.cloned.1.call-start = ((), (), s32[]{:S(2)}) async-start(), calls=%async_computation.1 | async-start | bytes 6684672 | tf_op jit(solution)/shard_map/reduce_scatter | solution.py:584
  15.3 0.7 slice-start
  15.3 0.7 slice-start.1
  15.3 0.7 slice-start.2
  15.3 4.6 %copy-start.7 = (bf16[1024]{0:T(1024)(128)(2,1)S(1)}, bf16[1024]{0:T(1024)(128)(2,1)}, u32[]{:S(2)}) copy-start(bf16[1024]{0:T(1024)(128)(2,1)} %param.27) | copy-start | bytes 6148
  15.3 5.2 %copy-start.8 = (s32[32]{0:T(128)S(1)}, s32[32]{0:T(128)}, u32[]{:S(2)}) copy-start(s32[32]{0:T(128)} %param.31) | copy-start | bytes 388
  16.0 5.4 %collective-permute-start = (bf16[8,1280]{1,0:T(8,128)(2,1)S(1)}, bf16[8,1280]{1,0:T(8,128)(2,1)S(1)}, u32[]{:S(2)}, u32[]{:S(2)}) collective-permute-start(bf16[8,1280]{1,0:T(8,128)(2,1)S(1)} %pad_maximum_fusion), channel_id=1, source_target_pairs={{0,8},{8,16},{16,24},{24,32},{32,40},{40,48},{48,56},{56,64},{64,7... | collective-permute-start | bytes 61448 | tf_op jit(solution)/shard_map/ppermute | solution.py:590
  21.4 0.6 copy-start.6
  102.7 6.3 %collective-permute-start.1 = (bf16[1,64,1536]{2,1,0:T(8,128)(2,1)S(1)}, bf16[1,64,1536]{2,1,0:T(8,128)(2,1)S(1)}, u32[]{:S(2)}, u32[]{:S(2)}) collective-permute-start(bf16[1,64,1536]{2,1,0:T(8,128)(2,1)S(1)} %slice.15), channel_id=1, source_target_pairs={{0,8},{8,16},{16,24},{24,32},{32,40},{40,48},{48,56},{56,64},{64,7... | collective-permute-start | bytes 589832 | tf_op jit(solution)/shard_map/ppermute | solution.py:597
  110.0 0.8 copy-start.1
  110.8 57.3 %copy-start.5 = (s32[8]{0:T(128)S(1)}, s32[8]{0:T(128)}, u32[]{:S(2)}) copy-start(s32[8]{0:T(128)} %fusion.slot_ref) | copy-start | bytes 100
  168.2 1.1 copy-start.2
  169.3 1.6 copy-start.3
  170.8 0.9 copy-start.4
Sparse Core Ops, SparseCore 0:
  15.5 86.2 reduce-scatter.1

commit v4 on v1

--- a/solution.py
+++ b/solution.py
@@ -11,6 +11,8 @@
 N = 128
 Q = 128
 TURN_DEV = 2
+PANEL_DEV = 6
+WAVE_LAG = 3
 LOG2E = 1.4426950408889634
 EPSILON = 1e-05
 VMEM_LIMIT = 60 * 1024 * 1024
@@ -217,9 +219,9 @@
         state_copy(c, 0).start()
     decay[0] = d_ref[...]
     decay[1] = jnp.ones_like(d_ref)
-    for wave in range(chunks + 3):
+    for wave in range(chunks + 3 * WAVE_LAG):
         for s in range(4):
-            c = wave - s
+            c = wave - WAVE_LAG * s
             if c < 0 or c >= chunks:
                 continue
             sl = slice(c * cw, c * cw + cw)
@@ -496,6 +498,30 @@
     )(slots, ylg, eg, cc, inc, gain, down, weight)
 
 
+def lay_out_kernel(place_ref, panel_ref, out_ref):
+    group = out_ref.shape[0]
+    for k in range(group):
+        place = place_ref[pl.program_id(0) * group + k]
+        here = jnp.logical_and(place >= 0, place < PANEL_DEV)
+        out_ref[k] = jnp.where(here, panel_ref[jnp.clip(place, 0, PANEL_DEV - 1)], 0)
+
+
+def lay_out(places, panels, group=8):
+    slots = places.shape[0]
+    shape = panels.shape[1:]
+    return pl.pallas_call(
+        lay_out_kernel,
+        grid_spec=pltpu.PrefetchScalarGridSpec(
+            num_scalar_prefetch=1,
+            grid=(slots // group,),
+            in_specs=[pl.BlockSpec(panels.shape, lambda i, s: (0, 0, 0))],
+            out_specs=pl.BlockSpec((group,) + shape, lambda i, s: (i, 0, 0)),
+        ),
+        out_shape=jax.ShapeDtypeStruct((slots,) + shape, BF16),
+        name="lay_out",
+    )(places, panels)
+
+
 def adapt_kernel(slot_ref, base_ref, low_ref, up_ref, out_ref):
     out_ref[...] = (base_ref[...] + dot_dims(low_ref[0], up_ref[0], 0, 0)).astype(BF16)
 
@@ -542,29 +568,37 @@
 ):
     tokens = input_x_channels.shape[0]
     own = lax.axis_index("ctx")
-    slot_turns = jnp.maximum(TURN_DEV * own - 1 + jnp.arange(TURN_DEV + 1), 0)
-    homes = jnp.take(tenant_panel_index, jnp.take(tenant_of_turn, slot_turns))
+    homes = jnp.take(tenant_panel_index, tenant_of_turn)
     starts = lax.dynamic_slice_in_dim(turn_first_token, TURN_DEV * own, TURN_DEV, 0)
-    places = own * tokens + Q * jnp.arange(tokens // Q)
-    slots = jnp.sum((places[:, None] >= starts[None, :]).astype(jnp.int32), axis=1)
-
-    all_down = lax.all_gather(adapter_down_panels.transpose(0, 2, 1), "ctx", axis=0, tiled=True)
-    all_up = lax.all_gather(adapter_up_panels, "ctx", axis=0, tiled=True)
-    down = jnp.take(all_down, homes, axis=0)
-    up = jnp.take(all_up, homes, axis=0)
+    firsts = own * tokens + Q * jnp.arange(tokens // Q)
+    slots = jnp.sum((firsts[:, None] >= starts[None, :]).astype(jnp.int32), axis=1)
+
+    places = homes - PANEL_DEV * own
+    offered = lay_out(places, adapter_down_panels.transpose(0, 2, 1))
+    count = lax.axis_size("ctx")
+    onward = [(i, i + 1) for i in range(count - 1)]
+    mine = lax.psum_scatter(offered, "ctx", scatter_dimension=0, tiled=True)
 
     tails = jnp.concatenate(
         [input_x_channels[tokens - 8 :], input_b_channels[tokens - 8 :], input_c_channels[tokens - 8 :]],
         axis=1,
     )
-    count = lax.axis_size("ctx")
-    halo = lax.ppermute(tails, "ctx", [(i, i + 1) for i in range(count - 1)])
+    halo = lax.ppermute(tails, "ctx", onward)
     ylg, eg, cc, state, decay = local_scan(
         input_x_channels, input_b_channels, input_c_channels, input_gate_channels, raw_step_sizes,
         log_decay_rate, head_skip_coeff, halo, x_conv_taps, b_conv_taps, c_conv_taps,
     )
     inc = exchange(state, decay)
+    mine, inc = lax.optimization_barrier((mine, inc))
+    before = lax.ppermute(mine[TURN_DEV - 1 :], "ctx", onward)
+    down = jnp.concatenate([before, mine], axis=0)
+    windows = [max(TURN_DEV * i - 1 + k, 0) for i in range(count) for k in range(TURN_DEV + 1)]
+    wanted, up_panels, mine = lax.optimization_barrier(
+        (jnp.take(places, jnp.array(windows)), adapter_up_panels, mine)
+    )
+    up = lax.psum_scatter(lay_out(wanted, up_panels), "ctx", scatter_dimension=0, tiled=True)
     base, low = project(slots, ylg, eg, cc, inc, gated_norm_gain.reshape(1, -1), down, output_weight)
+    up, base = lax.optimization_barrier((up, base))
     return adapt(slots, base, low, up)
 
 

time: 249 us -> 190 us (0.76)
  waiting for transfers between devices: 87.9 us -> 35.1 us
  local copies, waits for them, and re-layouts: 17.6 us -> 8.34 us
  starting transfers between devices: 3.93 us -> 7.05 us
    all_gather x2 -> x0, waiting for transfers between devices: 86.5 us -> none  [the longest x1 86.5 us: local(): lax.all_gather(adapter_down_panels.transpose(0, 2, 1), 'ctx', axis=0, til...]
    reduce_scatter x0 -> x1, waiting for transfers between devices: none -> 23.2 us  [local(): mine = lax.psum_scatter(offered, 'ctx', scatter_dimension=0, tiled=True)]
    optimization_barrier x0 -> x1, waiting for transfers between devices: none -> 10.6 us  [local(): up, base = lax.optimization_barrier((up, base))]
    pallas_call x1, Pallas kernels: 42.4 us -> 31.9 us  [exchange(): pl.pallas_call(functools.partial(exchange_kernel, chunks=chunks), in_spec...]
    pallas_call x0 -> x2, Pallas kernels: none -> 9.05 us  [lay_out(): pl.pallas_call(lay_out_kernel, grid_spec=pltpu.PrefetchScalarGridSpec(num...]
    gather x4 -> x2, local copies, waits for them, and re-layouts: 10.4 us -> 2.05 us  [the longest x1 1.36 us: local(): jnp.take(places, jnp.array(windows))]
    ppermute x1 -> x2, starting transfers between devices: 3.89 us -> 7 us  [the longest x1 3.91 us: local(): halo = lax.ppermute(tails, 'ctx', onward)]
  transfers between devices with their start and end apart: 3 -> 4, of which waited for: 1 -> 4; matrix products, arithmetic and copies ran while one was open for 4% -> 2% of each run, Pallas kernels for 25% -> 58%
where the time goes in v4:
time: 190 us
  Pallas kernels  123 us (65%)
  waiting for transfers between devices  35.1 us (18%)
  between operations  13.5 us (7%)
  local copies, waits for them, and re-layouts  8.34 us (4%)
  starting transfers between devices  7.05 us (4%)
  other arithmetic  3.31 us (2%)
    pallas_call x1, Pallas kernels, project(): pl.pallas_call(project_kernel, in_specs=[pl.BlockSpec(memory_space=pltpu....  57.4 us
    pallas_call x1, Pallas kernels, exchange(): pl.pallas_call(functools.partial(exchange_kernel, chunks=chunks), in_spec...  31.9 us
    reduce_scatter x1, waiting for transfers between devices, local(): mine = lax.psum_scatter(offered, 'ctx', scatter_dimension=0, tiled=True)  23.2 us
    pallas_call x1, Pallas kernels, local_scan(): pl.pallas_call(scan_kernel, grid=(tokens // Q,), in_specs=[smem, smem, ro...  20 us
    optimization_barrier x1, waiting for transfers between devices, local(): up, base = lax.optimization_barrier((up, base))  10.6 us
    pallas_call x2, Pallas kernels, lay_out(): pl.pallas_call(lay_out_kernel, grid_spec=pltpu.PrefetchScalarGridSpec(num...  9.05 us
    unnamed x22, local copies, waits for them, and re-layouts  4.98 us
    pallas_call x1, Pallas kernels, adapt(): pl.pallas_call(adapt_kernel, grid_spec=pltpu.PrefetchScalarGridSpec(num_s...  4.26 us
  transfers between devices with their start and end apart: 4, of which 4 were waited for; matrix products, arithmetic and copies ran while one was open for 2% of the time, Pallas kernels for 58%

profile of v4, /device:TPU:0, one launch (start us, length us, event | category | flops | bytes accessed | tf_op | source)
XLA Modules:
  0.0 189.9 jit_solution(12129405941775825502)
XLA Ops:
  6.5 0.7 compare_select_fusion
  7.2 0.7 gather_fusion
  7.9 1.2 fusion.1.place_ref
  9.1 4.5 %lay_out.2 = bf16[32,64,1024]{2,1,0:T(8,128)(2,1)} custom-call(s32[32]{0:T(128)} %fusion.1.place_ref, bf16[6,64,1024]{2,1,0:T(8,128)(2,1)} %bitcast.2), custom_call_target="tpu_custom_call" | custom-call | tf_op jit(solution)/shard_map/lay_out/pallas_call | solution.py:512
  13.6 0.0 copy-start.5
  13.6 0.0 reduce-scatter.5.cloned.1.call-update
  13.7 0.0 reduce-scatter.7.cloned.1.call-start
  13.7 0.6 slice-done
  14.3 3.9 %collective-permute-start = (bf16[8,1280]{1,0:T(8,128)(2,1)S(1)}, bf16[8,1280]{1,0:T(8,128)(2,1)S(1)}, u32[]{:S(2)}, u32[]{:S(2)}) collective-permute-start(bf16[8,1280]{1,0:T(8,128)(2,1)S(1)} %pad_maximum_fusion.1), channel_id=1, source_target_pairs={{0,8},{8,16},{16,24},{24,32},{32,40},{40,48},{48,56},{56,64},{64,7... | collective-permute-start | bytes 61448 | tf_op jit(solution)/shard_map/ppermute | solution.py:586
  18.2 0.0 copy-done.9
  18.3 1.4 gather_fusion.1
  19.6 0.1 collective-permute-done.halo_ref
  19.7 0.6 copy-done.7
  20.3 20.0 %local_scan.1 = (bf16[1024,1024]{1,0:T(8,128)(2,1)}, bf16[1024,1024]{1,0:T(8,128)(2,1)}, bf16[1024,128]{1,0:T(8,128)(2,1)}, f32[128,1024]{1,0:T(8,128)}, f32[8,1024]{1,0:T(8,128)}) custom-call(f32[16]{0:T(128)} %rate_ref.1, f32[16]{0:T(128)} %skip_ref.1, bf16[1024,1024]{1,0:T(8,128)(2,1)} %x_ref.1, bf16[1024,128]{1,0:T(8,128)(2,1)} %b_ref.1, ...), custom_call_target="tpu_custom_call" | custom-call | tf_op jit(solution)/shard_map/local_scan/pallas_call | solution.py:141
  40.4 31.9 %state_exchange.1.inc_ref = bf16[128,1024]{1,0:T(8,128)(2,1)} custom-call(f32[128,1024]{1,0:T(8,128)} %get-tuple-element.18.s_ref, f32[8,1024]{1,0:T(8,128)} %get-tuple-element.19.d_ref), custom_call_target="tpu_custom_call" | custom-call | tf_op jit(solution)/shard_map/state_exchange/pallas_call | solution.py:262
  72.3 23.2 %reduce-scatter.5.cloned.1.call-done = bf16[2,64,1024]{2,1,0:T(8,128)(2,1)} async-done(((bf16[32,64,1024]{2,1,0:T(8,128)(2,1)}), bf16[2,64,1024]{2,1,0:T(8,128)(2,1)}) %reduce-scatter.5.cloned.1.call-update) | async-done | bytes 262160 | tf_op jit(solution)/shard_map/reduce_scatter | solution.py:580
  95.5 4.5 %lay_out.3 = bf16[48,64,512]{2,1,0:T(8,128)(2,1)} custom-call(s32[48]{0:T(128)} %gather_fusion.1, bf16[6,64,512]{2,1,0:T(8,128)(2,1)} %panel_ref), custom_call_target="tpu_custom_call" | custom-call | tf_op jit(solution)/shard_map/lay_out/pallas_call | solution.py:512
  100.0 0.0 reduce-scatter.7.cloned.1.call-update
  100.1 0.9 copy-done.6
  101.0 3.1 %collective-permute-start.1 = (bf16[1,64,1024]{2,1,0:T(8,128)(2,1)S(1)}, bf16[1,64,1024]{2,1,0:T(8,128)(2,1)S(1)}, u32[]{:S(2)}, u32[]{:S(2)}) collective-permute-start(bf16[1,64,1024]{2,1,0:T(8,128)(2,1)S(1)} %slice.15), channel_id=1, source_target_pairs={{0,8},{8,16},{16,24},{24,32},{32,40},{40,48},{48,56},{56,64},{64,7... | collective-permute-start | bytes 393224 | tf_op jit(solution)/shard_map/ppermute | solution.py:593
  104.1 0.0 copy-done.8
  104.1 0.6 reshape.19.gain_ref
  104.7 0.1 dynamic_slice.3
  104.8 0.7 fusion.slot_ref
  105.5 1.1 collective-permute-done.1
  106.6 0.8 pad_maximum_fusion.down_ref
  107.4 57.4 %project.1 = (f32[1024,512]{1,0:T(8,128)}, bf16[8,64,128]{2,1,0:T(8,128)(2,1)}) custom-call(s32[8]{0:T(128)} %fusion.slot_ref, bf16[1024,1024]{1,0:T(8,128)(2,1)} %get-tuple-element.23.ylg_ref, bf16[1024,1024]{1,0:T(8,128)(2,1)} %get-tuple-element.24.eg_ref, bf16[1024,128]{1,0:T(8,128)(2,1)} %get-tuple-element.25.cc_ref, ...), custom_call_target="tpu_custom_call" | custom-call | tf_op jit(solution)/shard_map/project/pallas_call | solution.py:473
  164.8 10.6 %reduce-scatter.7.cloned.1.call-done.up_ref = bf16[3,64,512]{2,1,0:T(8,128)(2,1)} async-done(((bf16[48,64,512]{2,1,0:T(8,128)(2,1)}), bf16[3,64,512]{2,1,0:T(8,128)(2,1)}) %reduce-scatter.7.cloned.1.call-update) | async-done | bytes 196624 | tf_op jit(solution)/shard_map/optimization_barrier | solution.py:601
  175.4 1.6 copy-done.1
  177.0 0.9 copy-done.2
  177.9 0.9 copy-done.3
  178.8 4.3 %adapt.1 = bf16[1024,512]{1,0:T(8,128)(2,1)} custom-call(s32[8]{0:T(128)S(1)} %copy-done.4, f32[1024,512]{1,0:T(8,128)S(1)} %copy-done.1, bf16[8,64,128]{2,1,0:T(8,128)(2,1)S(1)} %copy-done.3, bf16[3,64,512]{2,1,0:T(8,128)(2,1)S(1)} %copy-done.2), custom_call_target="tpu_custom_call" | custom-call | tf_op jit(solution)/shard_map/adapt/pallas_call | solution.py:532
  (25 shorter events, 0.1 us)
Async XLA Ops:
  6.5 0.7 copy-start
  6.5 89.0 %reduce-scatter.5.cloned.1.call-start = ((), (), s32[]{:S(2)}) async-start(), calls=%async_computation.2 | async-start | bytes 4456448 | tf_op jit(solution)/shard_map/reduce_scatter | solution.py:580
  13.6 0.7 slice-start
  13.6 0.7 slice-start.1
  13.6 0.7 slice-start.2
  13.6 4.6 %copy-start.9 = (s32[48]{0:T(128)S(1)}, s32[48]{0:T(128)}, u32[]{:S(2)}) copy-start(s32[48]{0:T(128)} %constant.59) | copy-start | bytes 580
  13.6 4.7 %copy-start.5 = (s32[32]{0:T(128)S(1)}, s32[32]{0:T(128)}, u32[]{:S(2)}) copy-start(s32[32]{0:T(128)} %fusion.1.place_ref) | copy-start | bytes 388
  13.7 161.8 %reduce-scatter.7.cloned.1.call-start = ((), (), s32[]{:S(2)}) async-start(), calls=%async_computation.3 | async-start | bytes 3342336
  14.3 5.4 %collective-permute-start = (bf16[8,1280]{1,0:T(8,128)(2,1)S(1)}, bf16[8,1280]{1,0:T(8,128)(2,1)S(1)}, u32[]{:S(2)}, u32[]{:S(2)}) collective-permute-start(bf16[8,1280]{1,0:T(8,128)(2,1)S(1)} %pad_maximum_fusion.1), channel_id=1, source_target_pairs={{0,8},{8,16},{16,24},{24,32},{32,40},{40,48},{48,56},{56,64},{64,7... | collective-permute-start | bytes 61448 | tf_op jit(solution)/shard_map/ppermute | solution.py:586
  19.7 0.6 copy-start.7
  100.0 0.9 copy-start.6
  100.0 4.1 %copy-start.8 = (bf16[1024]{0:T(1024)(128)(2,1)S(1)}, bf16[1024]{0:T(1024)(128)(2,1)}, u32[]{:S(2)}) copy-start(bf16[1024]{0:T(1024)(128)(2,1)} %param.28) | copy-start | bytes 6148
  100.0 4.7 %copy-start.10 = (s32[32]{0:T(128)S(1)}, s32[32]{0:T(128)}, u32[]{:S(2)}) copy-start(s32[32]{0:T(128)} %param.32) | copy-start | bytes 388
  101.0 5.6 %collective-permute-start.1 = (bf16[1,64,1024]{2,1,0:T(8,128)(2,1)S(1)}, bf16[1,64,1024]{2,1,0:T(8,128)(2,1)S(1)}, u32[]{:S(2)}, u32[]{:S(2)}) collective-permute-start(bf16[1,64,1024]{2,1,0:T(8,128)(2,1)S(1)} %slice.15), channel_id=1, source_target_pairs={{0,8},{8,16},{16,24},{24,32},{32,40},{40,48},{48,56},{56,64},{64,7... | collective-permute-start | bytes 393224 | tf_op jit(solution)/shard_map/ppermute | solution.py:593
  107.4 68.0 %copy-start.4 = (s32[8]{0:T(128)S(1)}, s32[8]{0:T(128)}, u32[]{:S(2)}) copy-start(s32[8]{0:T(128)} %fusion.slot_ref) | copy-start | bytes 100
  175.4 1.6 copy-start.1
  177.0 0.9 copy-start.2
  177.9 0.9 copy-start.3
Sparse Core Ops, SparseCore 0:
  13.8 81.6 reduce-scatter.4
  100.2 75.1 reduce-scatter.6

commit v5 on v1

--- a/solution.py
+++ b/solution.py
@@ -11,6 +11,8 @@
 N = 128
 Q = 128
 TURN_DEV = 2
+PANEL_DEV = 6
+WAVE_LAG = 3
 LOG2E = 1.4426950408889634
 EPSILON = 1e-05
 VMEM_LIMIT = 60 * 1024 * 1024
@@ -217,9 +219,9 @@
         state_copy(c, 0).start()
     decay[0] = d_ref[...]
     decay[1] = jnp.ones_like(d_ref)
-    for wave in range(chunks + 3):
+    for wave in range(chunks + 3 * WAVE_LAG):
         for s in range(4):
-            c = wave - s
+            c = wave - WAVE_LAG * s
             if c < 0 or c >= chunks:
                 continue
             sl = slice(c * cw, c * cw + cw)
@@ -286,10 +288,10 @@
 
 
 def project_kernel(
-    slot_ref, ylg_ref, eg_ref, cc_ref, inc_ref, gain_ref, down_ref, w_ref,
-    base_ref, low_ref,
-    wv, own, psend, precv, rsend, rrecv, lsend, lrecv, lout,
-    sem_w, sem_ps, sem_pr, sem_rs, sem_rr, sem_ls, sem_lr, sem_as, sem_ar,
+    ylg_ref, eg_ref, cc_ref, inc_ref, gain_ref, w_ref,
+    base_ref, normed_ref,
+    wv, own, psend, precv, rsend, rrecv,
+    sem_w, sem_ps, sem_pr, sem_rs, sem_rr,
 ):
     head = lax.axis_index("head")
     y, core = head // 2, head % 2
@@ -328,34 +330,6 @@
             device_id={"head": to * 2 + core}, device_id_type=MESH,
         )
 
-    def low_copy(b):
-        return pltpu.make_async_remote_copy(
-            src_ref=lsend.at[b], dst_ref=lrecv.at[head],
-            send_sem=sem_ls.at[b], recv_sem=sem_lr.at[head],
-            device_id={"head": b}, device_id_type=MESH,
-        )
-
-    def low_arrival(k):
-        return pltpu.make_async_remote_copy(
-            src_ref=lsend.at[k], dst_ref=lrecv.at[k],
-            send_sem=sem_ls.at[k], recv_sem=sem_lr.at[k],
-            device_id={"head": k}, device_id_type=MESH,
-        )
-
-    def sum_copy(k):
-        return pltpu.make_async_remote_copy(
-            src_ref=lout.at[head], dst_ref=lout.at[head],
-            send_sem=sem_as.at[k], recv_sem=sem_ar.at[head],
-            device_id={"head": k}, device_id_type=MESH,
-        )
-
-    def sum_arrival(k):
-        return pltpu.make_async_remote_copy(
-            src_ref=lout.at[k], dst_ref=lout.at[k],
-            send_sem=sem_as.at[k], recv_sem=sem_ar.at[k],
-            device_id={"head": k}, device_id_type=MESH,
-        )
-
     pl.semaphore_wait(barrier, 7)
 
     def compute(b):
@@ -364,6 +338,7 @@
         gated = ylg_ref[rows, :].astype(F32) + eg_ref[rows, :].astype(F32) * got
         scale = lax.rsqrt(jnp.mean(gated * gated, axis=1, keepdims=True) + EPSILON)
         normed = (gated * scale * gain_ref[...].astype(F32)).astype(BF16)
+        normed_ref[rows, :] = normed
         for d in dests:
             @pl.when(b == 0)
             def _():
@@ -375,16 +350,6 @@
             def _():
                 w_copy(d, core).wait()
             own[b, d] = dot(normed, wv[d * 2 + core])
-        low = dot_dims(down_ref[slot_ref[b]], normed, 1, 1).astype(BF16)
-        lsend[b] = low
-
-        @pl.when(b == head)
-        def _():
-            lrecv[b] = low
-
-        @pl.when(b != head)
-        def _():
-            low_copy(b).start()
 
     def ring(b, j):
         if j == 0:
@@ -408,20 +373,6 @@
                 at = pl.multiple_of(b * Q + way * half, half)
                 base_ref[pl.ds(at, half), :] = value
 
-    def sum_low():
-        for k in range(8):
-            @pl.when(k != head)
-            def _():
-                low_arrival(k).wait_recv()
-        total = lrecv[0].astype(F32)
-        for k in range(1, 8):
-            total = total + lrecv[k].astype(F32)
-        lout[head] = total.astype(BF16)
-        for k in range(8):
-            @pl.when(k != head)
-            def _():
-                sum_copy(k).start()
-
     def tick(t, carry):
         @pl.when(t < blocks)
         def _():
@@ -434,21 +385,9 @@
             def _():
                 ring(b, j)
 
-        @pl.when(t == blocks + 1)
-        def _():
-            sum_low()
-
         return carry
 
     lax.fori_loop(0, blocks + LAG[3], tick, 0)
-
-    for k in range(8):
-        @pl.when(k != head)
-        def _():
-            sum_arrival(k).wait_recv()
-            low_copy(k).wait_send()
-            sum_copy(k).wait_send()
-    low_ref[...] = lout[...]
 
     def drain(b, carry):
         for d in range(4):
@@ -461,20 +400,19 @@
     lax.fori_loop(0, blocks, drain, 0)
 
 
-def project(slots, ylg, eg, cc, inc, gain, down, weight):
+def project(ylg, eg, cc, inc, gain, weight):
     tokens, width = ylg.shape
     feat = weight.shape[1] // 8
-    rank = down.shape[1]
     blocks = tokens // Q
     vmem = pl.BlockSpec(memory_space=pltpu.VMEM)
     dma = pltpu.SemaphoreType.DMA
     return pl.pallas_call(
         project_kernel,
-        in_specs=[pl.BlockSpec(memory_space=pltpu.SMEM)] + [vmem] * 6 + [pl.BlockSpec(memory_space=pl.ANY)],
+        in_specs=[vmem] * 5 + [pl.BlockSpec(memory_space=pl.ANY)],
         out_specs=[vmem, vmem],
         out_shape=[
             jax.ShapeDtypeStruct((tokens, feat), F32),
-            jax.ShapeDtypeStruct((blocks, rank, Q), BF16),
+            jax.ShapeDtypeStruct((tokens, width), BF16),
         ],
         scratch_shapes=[
             pltpu.VMEM((8, width, feat), BF16),
@@ -483,17 +421,141 @@
             pltpu.VMEM((blocks, 4, Q, feat), BF16),
             pltpu.VMEM((blocks, 3, 2, Q // 2, feat), BF16),
             pltpu.VMEM((blocks, 3, 2, Q // 2, feat), BF16),
-            pltpu.VMEM((8, rank, Q), BF16),
-            pltpu.VMEM((8, rank, Q), BF16),
-            pltpu.VMEM((8, rank, Q), BF16),
             dma((8,)), dma((blocks, 4)), dma((blocks, 4)), dma((blocks, 3, 2)), dma((blocks, 3, 2)),
-            dma((8,)), dma((8,)), dma((8,)), dma((8,)),
         ],
         compiler_params=pltpu.CompilerParams(
             collective_id=2, has_side_effects=True, vmem_limit_bytes=VMEM_LIMIT
         ),
         name="project",
-    )(slots, ylg, eg, cc, inc, gain, down, weight)
+    )(ylg, eg, cc, inc, gain, weight)
+
+
+def lowrank_kernel(
+    slot_ref, normed_ref, panel_ref, low_ref, lsend, lrecv, lout, sem_ls, sem_lr, sem_as, sem_ar
+):
+    head = lax.axis_index("head")
+    width = normed_ref.shape[1]
+    barrier = pltpu.get_barrier_semaphore()
+    for k in range(1, 8):
+        pl.semaphore_signal(
+            barrier, inc=1, device_id={"head": (head + k) % 8}, device_id_type=MESH
+        )
+
+    def low_copy(b):
+        return pltpu.make_async_remote_copy(
+            src_ref=lsend.at[b], dst_ref=lrecv.at[head],
+            send_sem=sem_ls.at[b], recv_sem=sem_lr.at[head],
+            device_id={"head": b}, device_id_type=MESH,
+        )
+
+    def low_arrival(k):
+        return pltpu.make_async_remote_copy(
+            src_ref=lsend.at[k], dst_ref=lrecv.at[k],
+            send_sem=sem_ls.at[k], recv_sem=sem_lr.at[k],
+            device_id={"head": k}, device_id_type=MESH,
+        )
+
+    def sum_copy(k):
+        return pltpu.make_async_remote_copy(
+            src_ref=lout.at[head], dst_ref=lout.at[head],
+            send_sem=sem_as.at[k], recv_sem=sem_ar.at[head],
+            device_id={"head": k}, device_id_type=MESH,
+        )
+
+    def sum_arrival(k):
+        return pltpu.make_async_remote_copy(
+            src_ref=lout.at[k], dst_ref=lout.at[k],
+            send_sem=sem_as.at[k], recv_sem=sem_ar.at[k],
+            device_id={"head": k}, device_id_type=MESH,
+        )
+
+    pl.semaphore_wait(barrier, 7)
+    for b in range(8):
+        low = dot_dims(
+            panel_ref[slot_ref[b], :, 0:width], normed_ref[b * Q : b * Q + Q, :], 1, 1
+        ).astype(BF16)
+        lsend[b] = low
+
+        @pl.when(b == head)
+        def _():
+            lrecv[b] = low
+
+        @pl.when(b != head)
+        def _():
+            low_copy(b).start()
+
+    for k in range(8):
+        @pl.when(k != head)
+        def _():
+            low_arrival(k).wait_recv()
+    total = lrecv[0].astype(F32)
+    for k in range(1, 8):
+        total = total + lrecv[k].astype(F32)
+    lout[head] = total.astype(BF16)
+    for k in range(8):
+        @pl.when(k != head)
+        def _():
+            sum_copy(k).start()
+
+    for k in range(8):
+        @pl.when(k != head)
+        def _():
+            sum_arrival(k).wait_recv()
+            low_copy(k).wait_send()
+            sum_copy(k).wait_send()
+    low_ref[...] = lout[...]
+
+
+def lowrank(slots, normed, panels):
+    rank = panels.shape[1]
+    vmem = pl.BlockSpec(memory_space=pltpu.VMEM)
+    dma = pltpu.SemaphoreType.DMA
+    return pl.pallas_call(
+        lowrank_kernel,
+        in_specs=[pl.BlockSpec(memory_space=pltpu.SMEM), vmem, vmem],
+        out_specs=vmem,
+        out_shape=jax.ShapeDtypeStruct((8, rank, Q), BF16),
+        scratch_shapes=[pltpu.VMEM((8, rank, Q), BF16)] * 3 + [dma((8,))] * 4,
+        compiler_params=pltpu.CompilerParams(
+            collective_id=3, has_side_effects=True, vmem_limit_bytes=16 * 1024 * 1024
+        ),
+        name="lowrank",
+    )(slots, normed, panels)
+
+
+SLOTS = TURN_DEV + 1
+
+
+def lay_out_kernel(tenant_ref, index_ref, down_ref, up_ref, out_ref):
+    group, width = out_ref.shape[0], down_ref.shape[2]
+    first = PANEL_DEV * lax.axis_index("ctx")
+    for k in range(group):
+        device = pl.program_id(0) * (group // SLOTS) + k // SLOTS
+        turn = jnp.maximum(TURN_DEV * device - 1 + k % SLOTS, 0)
+        place = index_ref[tenant_ref[turn]] - first
+        here = jnp.logical_and(place >= 0, place < PANEL_DEV)
+        at = jnp.clip(place, 0, PANEL_DEV - 1)
+        out_ref[k, :, 0:width] = jnp.where(here, down_ref[at], 0)
+        out_ref[k, :, width:] = jnp.where(here, up_ref[at], 0)
+
+
+def lay_out(tenants, index, down, up, devices, group=2 * SLOTS):
+    rank, width = down.shape[1:]
+    total = width + up.shape[2]
+    return pl.pallas_call(
+        lay_out_kernel,
+        grid_spec=pltpu.PrefetchScalarGridSpec(
+            num_scalar_prefetch=2,
+            grid=(devices * SLOTS // group,),
+            in_specs=[
+                pl.BlockSpec(down.shape, lambda i, *s: (0, 0, 0)),
+                pl.BlockSpec(up.shape, lambda i, *s: (0, 0, 0)),
+            ],
+            out_specs=pl.BlockSpec((group, rank, total), lambda i, *s: (i, 0, 0)),
+        ),
+        out_shape=jax.ShapeDtypeStruct((devices * SLOTS, rank, total), BF16),
+        name="lay_out",
+    )(tenants, index, down, up)
 
 
 def adapt_kernel(slot_ref, base_ref, low_ref, up_ref, out_ref):
@@ -511,7 +573,7 @@
             in_specs=[
                 pl.BlockSpec((Q, feat), lambda i, s: (i, 0)),
                 pl.BlockSpec((1, rank, Q), lambda i, s: (i, 0, 0)),
-                pl.BlockSpec((1, rank, feat), lambda i, s: (s[i], 0, 0)),
+                pl.BlockSpec((1, rank, feat), lambda i, s: (s[i], 0, up.shape[2] // feat - 1)),
             ],
             out_specs=pl.BlockSpec((Q, feat), lambda i, s: (i, 0)),
         ),
@@ -542,30 +604,31 @@
 ):
     tokens = input_x_channels.shape[0]
     own = lax.axis_index("ctx")
-    slot_turns = jnp.maximum(TURN_DEV * own - 1 + jnp.arange(TURN_DEV + 1), 0)
-    homes = jnp.take(tenant_panel_index, jnp.take(tenant_of_turn, slot_turns))
     starts = lax.dynamic_slice_in_dim(turn_first_token, TURN_DEV * own, TURN_DEV, 0)
-    places = own * tokens + Q * jnp.arange(tokens // Q)
-    slots = jnp.sum((places[:, None] >= starts[None, :]).astype(jnp.int32), axis=1)
-
-    all_down = lax.all_gather(adapter_down_panels.transpose(0, 2, 1), "ctx", axis=0, tiled=True)
-    all_up = lax.all_gather(adapter_up_panels, "ctx", axis=0, tiled=True)
-    down = jnp.take(all_down, homes, axis=0)
-    up = jnp.take(all_up, homes, axis=0)
+    firsts = own * tokens + Q * jnp.arange(tokens // Q)
+    slots = jnp.sum((firsts[:, None] >= starts[None, :]).astype(jnp.int32), axis=1)
+
+    count = lax.axis_size("ctx")
+    offered = lay_out(
+        tenant_of_turn, tenant_panel_index,
+        adapter_down_panels.transpose(0, 2, 1), adapter_up_panels, count,
+    )
+    panels = lax.psum_scatter(offered, "ctx", scatter_dimension=0, tiled=True)
 
     tails = jnp.concatenate(
         [input_x_channels[tokens - 8 :], input_b_channels[tokens - 8 :], input_c_channels[tokens - 8 :]],
         axis=1,
     )
-    count = lax.axis_size("ctx")
     halo = lax.ppermute(tails, "ctx", [(i, i + 1) for i in range(count - 1)])
     ylg, eg, cc, state, decay = local_scan(
         input_x_channels, input_b_channels, input_c_channels, input_gate_channels, raw_step_sizes,
         log_decay_rate, head_skip_coeff, halo, x_conv_taps, b_conv_taps, c_conv_taps,
     )
     inc = exchange(state, decay)
-    base, low = project(slots, ylg, eg, cc, inc, gated_norm_gain.reshape(1, -1), down, output_weight)
-    return adapt(slots, base, low, up)
+    base, normed = project(ylg, eg, cc, inc, gated_norm_gain.reshape(1, -1), output_weight)
+    panels, normed = lax.optimization_barrier((panels, normed))
+    low = lowrank(slots, normed, panels)
+    return adapt(slots, base, low, panels)
 
 
 def solution(mesh):

time: 249 us -> 160 us (0.64)
  waiting for transfers between devices: 87.9 us -> 0.72 us
  local copies, waits for them, and re-layouts: 17.6 us -> 4.62 us
  Pallas kernels: 124 us -> 136 us
    all_gather x2 -> x0, waiting for transfers between devices: 86.5 us -> none  [the longest x1 86.5 us: local(): lax.all_gather(adapter_down_panels.transpose(0, 2, 1), 'ctx', axis=0, til...]
    pallas_call x1 -> x3, Pallas kernels: 57.3 us -> 75.3 us  [the longest x1 55.4 us: project(): pl.pallas_call(project_kernel, in_specs=[vmem] * 5 + [pl.BlockSpec(memory...]
    gather x4 -> x0, local copies, waits for them, and re-layouts: 10.4 us -> none  [the longest x1 5.15 us: local(): down = jnp.take(all_down, homes, axis=0)]
    pallas_call x1, Pallas kernels: 42.4 us -> 35.8 us  [exchange(): pl.pallas_call(functools.partial(exchange_kernel, chunks=chunks), in_spec...]
  transfers between devices with their start and end apart: 3 -> 2, of which waited for: 1 -> 1; matrix products, arithmetic and copies ran while one was open for 4% -> 0% of each run, Pallas kernels for 25% -> 70%
where the time goes in v5:
time: 160 us; the launch traced here: 158 us
  Pallas kernels  136 us (85%)
  between operations  13.5 us (8%)
  local copies, waits for them, and re-layouts  4.62 us (3%)
  starting transfers between devices  3.91 us (2%)
    pallas_call x1, Pallas kernels, project(): pl.pallas_call(project_kernel, in_specs=[vmem] * 5 + [pl.BlockSpec(memory...  55.4 us
    pallas_call x1, Pallas kernels, exchange(): pl.pallas_call(functools.partial(exchange_kernel, chunks=chunks), in_spec...  35.8 us
    pallas_call x1, Pallas kernels, local_scan(): pl.pallas_call(scan_kernel, grid=(tokens // Q,), in_specs=[smem, smem, ro...  20.1 us
    pallas_call x1, Pallas kernels, lowrank(): pl.pallas_call(lowrank_kernel, in_specs=[pl.BlockSpec(memory_space=pltpu....  12.8 us
    pallas_call x1, Pallas kernels, lay_out(): pl.pallas_call(lay_out_kernel, grid_spec=pltpu.PrefetchScalarGridSpec(num...  7.18 us
    pallas_call x1, Pallas kernels, adapt(): pl.pallas_call(adapt_kernel, grid_spec=pltpu.PrefetchScalarGridSpec(num_s...  4.31 us
    ppermute x1, starting transfers between devices, local(): halo = lax.ppermute(tails, 'ctx', [(i, i + 1) for i in range(count - 1)])  3.91 us
    unnamed x12, local copies, waits for them, and re-layouts  3.27 us
  transfers between devices with their start and end apart: 2, of which 1 were waited for; matrix products, arithmetic and copies ran while one was open for 0% of the time, Pallas kernels for 70%

profile of v5, /device:TPU:0, one launch (start us, length us, event | category | flops | bytes accessed | tf_op | source)
XLA Modules:
  0.0 158.3 jit_solution(7660591955144530425)
XLA Ops:
  6.5 0.0 reduce-scatter.4.cloned.1.call-start
  6.5 7.2 %lay_out.1 = bf16[48,64,1536]{2,1,0:T(8,128)(2,1)} custom-call(s32[32]{0:T(128)} %tenant_ref.1, s32[96]{0:T(128)} %index_ref.1, bf16[6,64,1024]{2,1,0:T(8,128)(2,1)} %bitcast.2, bf16[6,64,512]{2,1,0:T(8,128)(2,1)} %up_ref.1), custom_call_target="tpu_custom_call" | custom-call | tf_op jit(solution)/shard_map/lay_out/pallas_call | solution.py:545
  13.7 0.0 slice-start
  13.7 0.0 slice-start.1
  13.7 0.0 slice-start.2
  13.7 0.0 copy-start.5
  13.7 0.0 copy-start.4
  13.7 0.0 reduce-scatter.4.cloned.1.call-update
  13.8 0.7 slice-done
  14.4 0.0 slice-done.1
  14.4 0.0 slice-done.2
  14.4 3.9 %collective-permute-start = (bf16[8,1280]{1,0:T(8,128)(2,1)S(1)}, bf16[8,1280]{1,0:T(8,128)(2,1)S(1)}, u32[]{:S(2)}, u32[]{:S(2)}) collective-permute-start(bf16[8,1280]{1,0:T(8,128)(2,1)S(1)} %pad_maximum_fusion), channel_id=1, source_target_pairs={{0,8},{8,16},{16,24},{24,32},{32,40},{40,48},{48,56},{56,64},{64,7... | collective-permute-start | bytes 61448 | tf_op jit(solution)/shard_map/ppermute | solution.py:622
  18.4 0.0 copy-done.5
  18.4 0.1 dynamic_slice.3
  18.5 0.1 fusion.slot_ref
  18.5 0.0 copy-done.4
  18.5 0.6 reshape.9.gain_ref
  19.1 0.7 collective-permute-done.halo_ref
  19.8 0.0 copy-start.3
  19.8 0.6 copy-done.3
  20.4 20.1 %local_scan.1 = (bf16[1024,1024]{1,0:T(8,128)(2,1)}, bf16[1024,1024]{1,0:T(8,128)(2,1)}, bf16[1024,128]{1,0:T(8,128)(2,1)}, f32[128,1024]{1,0:T(8,128)}, f32[8,1024]{1,0:T(8,128)}) custom-call(f32[16]{0:T(128)} %rate_ref.1, f32[16]{0:T(128)} %skip_ref.1, bf16[1024,1024]{1,0:T(8,128)(2,1)} %x_ref.1, bf16[1024,128]{1,0:T(8,128)(2,1)} %b_ref.1, ...), custom_call_target="tpu_custom_call" | custom-call | tf_op jit(solution)/shard_map/local_scan/pallas_call | solution.py:141
  40.5 35.8 %state_exchange.1.inc_ref = bf16[128,1024]{1,0:T(8,128)(2,1)} custom-call(f32[128,1024]{1,0:T(8,128)} %get-tuple-element.17.s_ref, f32[8,1024]{1,0:T(8,128)} %get-tuple-element.18.d_ref), custom_call_target="tpu_custom_call" | custom-call | tf_op jit(solution)/shard_map/state_exchange/pallas_call | solution.py:262
  76.4 55.4 %project.1 = (f32[1024,512]{1,0:T(8,128)}, bf16[1024,1024]{1,0:T(8,128)(2,1)}) custom-call(bf16[1024,1024]{1,0:T(8,128)(2,1)} %get-tuple-element.14.ylg_ref, bf16[1024,1024]{1,0:T(8,128)(2,1)} %get-tuple-element.15.eg_ref, bf16[1024,128]{1,0:T(8,128)(2,1)} %get-tuple-element.16.cc_ref, bf16[128,1024]{1,0:T(8,128)(2,1)} %state_exchange.1.inc_ref, ...), custom_call_target="tpu_custom_call" | custom-call | tf_op jit(solution)/shard_map/project/pallas_call | solution.py:409
  131.7 0.0 reduce-scatter.4.cloned.1.call-done.panel_ref.up_ref
  131.8 0.0 copy-start
  131.8 1.1 copy-done
  132.8 0.0 copy-start.2
  132.8 1.6 %copy-done.2 = bf16[1024,1024]{1,0:T(8,128)(2,1)S(1)} copy-done((bf16[1024,1024]{1,0:T(8,128)(2,1)S(1)}, bf16[1024,1024]{1,0:T(8,128)(2,1)}, u32[]{:S(2)}) %copy-start.2) | copy-done | bytes 2097176
  134.4 0.0 copy-start.1
  134.4 12.8 %lowrank.1.low_ref = bf16[8,64,128]{2,1,0:T(8,128)(2,1)S(1)} custom-call(s32[8]{0:T(128)S(1)} %fusion.slot_ref, bf16[1024,1024]{1,0:T(8,128)(2,1)S(1)} %copy-done.2, bf16[3,64,1536]{2,1,0:T(8,128)(2,1)S(1)} %copy-done), custom_call_target="tpu_custom_call" | custom-call | tf_op jit(solution)/shard_map/lowrank/pallas_call | solution.py:513
  147.2 0.0 copy-done.1
  147.2 4.3 %adapt.1 = bf16[1024,512]{1,0:T(8,128)(2,1)} custom-call(s32[8]{0:T(128)S(1)} %fusion.slot_ref, f32[1024,512]{1,0:T(8,128)S(1)} %copy-done.1, bf16[8,64,128]{2,1,0:T(8,128)(2,1)S(1)} %lowrank.1.low_ref, bf16[3,64,1536]{2,1,0:T(8,128)(2,1)S(1)} %copy-done), custom_call_target="tpu_custom_call" | custom-call | tf_op jit(solution)/shard_map/adapt/pallas_call | solution.py:568
  (2 shorter events, 0.0 us)
Async XLA Ops:
  6.5 125.2 %reduce-scatter.4.cloned.1.call-start = ((), (), s32[]{:S(2)}) async-start(), calls=%async_computation.1 | async-start | bytes 10027008
  13.7 0.7 slice-start
  13.7 0.7 slice-start.1
  13.7 0.7 slice-start.2
  13.7 4.6 %copy-start.5 = (s32[32]{0:T(128)S(1)}, s32[32]{0:T(128)}, u32[]{:S(2)}) copy-start(s32[32]{0:T(128)} %param.31) | copy-start | bytes 388
  13.7 4.8 %copy-start.4 = (bf16[1024]{0:T(1024)(128)(2,1)S(1)}, bf16[1024]{0:T(1024)(128)(2,1)}, u32[]{:S(2)}) copy-start(bf16[1024]{0:T(1024)(128)(2,1)} %param.27) | copy-start | bytes 6148
  14.4 5.4 %collective-permute-start = (bf16[8,1280]{1,0:T(8,128)(2,1)S(1)}, bf16[8,1280]{1,0:T(8,128)(2,1)S(1)}, u32[]{:S(2)}, u32[]{:S(2)}) collective-permute-start(bf16[8,1280]{1,0:T(8,128)(2,1)S(1)} %pad_maximum_fusion), channel_id=1, source_target_pairs={{0,8},{8,16},{16,24},{24,32},{32,40},{40,48},{48,56},{56,64},{64,7... | collective-permute-start | bytes 61448 | tf_op jit(solution)/shard_map/ppermute | solution.py:622
  19.8 0.6 copy-start.3
  131.8 1.1 copy-start
  132.8 1.6 %copy-start.2 = (bf16[1024,1024]{1,0:T(8,128)(2,1)S(1)}, bf16[1024,1024]{1,0:T(8,128)(2,1)}, u32[]{:S(2)}) copy-start(bf16[1024,1024]{1,0:T(8,128)(2,1)} %get-tuple-element.21.normed_ref) | copy-start | bytes 6291460
  134.4 12.8 %copy-start.1 = (f32[1024,512]{1,0:T(8,128)S(1)}, f32[1024,512]{1,0:T(8,128)}, u32[]{:S(2)}) copy-start(f32[1024,512]{1,0:T(8,128)} %get-tuple-element.19.base_ref) | copy-start | bytes 6291460
Sparse Core Ops, SparseCore 0:
  13.9 96.5 reduce-scatter.3

commit v6 on v5

--- a/solution.py
+++ b/solution.py
@@ -284,14 +284,14 @@
     )(state, decay)
 
 
-LAG = (1, 2, 3, 4)
+LAG = (1, 2, 3)
 
 
 def project_kernel(
     ylg_ref, eg_ref, cc_ref, inc_ref, gain_ref, w_ref,
     base_ref, normed_ref,
-    wv, own, psend, precv, rsend, rrecv,
-    sem_w, sem_ps, sem_pr, sem_rs, sem_rr,
+    wv, own, psend, precv, hsend, hrecv, fsend, frecv,
+    sem_w, sem_ps, sem_pr, sem_hs, sem_hr, sem_fs, sem_fr,
 ):
     head = lax.axis_index("head")
     y, core = head // 2, head % 2
@@ -304,7 +304,7 @@
             barrier, inc=1, device_id={"head": (head + k) % 8}, device_id_type=MESH
         )
 
-    dests = [(y + 3) % 4, (y + 1) % 4, (y + 2) % 4, y]
+    dests = [(y + 2) % 4, (y + 1) % 4, (y + 3) % 4, y]
 
     def w_copy(d, side):
         index = d * 2 + side
@@ -322,12 +322,18 @@
             device_id={"head": y * 2 + 1 - core}, device_id_type=MESH,
         )
 
-    def ring_copy(b, j, way):
-        to = (y + 1 + 2 * way) % 4
-        return pltpu.make_async_remote_copy(
-            src_ref=rsend.at[b, j, way], dst_ref=rrecv.at[b, j, way],
-            send_sem=sem_rs.at[b, j, way], recv_sem=sem_rr.at[b, j, way],
-            device_id={"head": to * 2 + core}, device_id_type=MESH,
+    def half_copy(b, way):
+        return pltpu.make_async_remote_copy(
+            src_ref=hsend.at[b, way], dst_ref=hrecv.at[b, way],
+            send_sem=sem_hs.at[b, way], recv_sem=sem_hr.at[b, way],
+            device_id={"head": (y + 1 + 2 * way) % 4 * 2 + core}, device_id_type=MESH,
+        )
+
+    def full_copy(b, way):
+        return pltpu.make_async_remote_copy(
+            src_ref=fsend.at[b, way], dst_ref=frecv.at[b, way],
+            send_sem=sem_fs.at[b, way], recv_sem=sem_fr.at[b, way],
+            device_id={"head": (y + 1 + 2 * way) % 4 * 2 + core}, device_id_type=MESH,
         )
 
     pl.semaphore_wait(barrier, 7)
@@ -351,34 +357,40 @@
                 w_copy(d, core).wait()
             own[b, d] = dot(normed, wv[d * 2 + core])
 
+    def mixed(b, d, part):
+        return own[b, d, part, :] + precv[b, d, part, :].astype(F32)
+
     def ring(b, j):
+        parts = [slice(0, half), slice(half, Q)]
         if j == 0:
             pair_copy(b, dests[0]).wait_recv()
-            pair_copy(b, dests[1]).wait_recv()
+            for way in range(2):
+                hsend[b, way] = mixed(b, dests[0], parts[way]).astype(BF16)
+                half_copy(b, way).start()
         elif j == 1:
-            pair_copy(b, dests[2]).wait_recv()
-        elif j == 3:
+            for way in range(2):
+                d = dests[1 + way]
+                pair_copy(b, d).wait_recv()
+                half_copy(b, way).wait_recv()
+                added = mixed(b, d, parts[way]) + hrecv[b, way].astype(F32)
+                fsend[b, way, parts[way], :] = added.astype(BF16)
+                fsend[b, way, parts[1 - way], :] = mixed(b, d, parts[1 - way]).astype(BF16)
+                full_copy(b, way).start()
+        else:
             pair_copy(b, dests[3]).wait_recv()
-        for way in range(2):
-            d = (y + (j + 1) * (3 - 2 * way)) % 4
-            part = slice(way * half, way * half + half)
-            value = own[b, d, part, :] + precv[b, d, part, :].astype(F32)
-            if j > 0:
-                ring_copy(b, j - 1, way).wait_recv()
-                value = value + rrecv[b, j - 1, way].astype(F32)
-            if j < 3:
-                rsend[b, j, way] = value.astype(BF16)
-                ring_copy(b, j, way).start()
-            else:
-                at = pl.multiple_of(b * Q + way * half, half)
-                base_ref[pl.ds(at, half), :] = value
+            full_copy(b, 0).wait_recv()
+            full_copy(b, 1).wait_recv()
+            at = pl.multiple_of(b * Q, Q)
+            base_ref[pl.ds(at, Q), :] = (
+                mixed(b, y, slice(0, Q)) + frecv[b, 0].astype(F32) + frecv[b, 1].astype(F32)
+            )
 
     def tick(t, carry):
         @pl.when(t < blocks)
         def _():
             compute(t)
 
-        for j in range(4):
+        for j in range(3):
             b = t - LAG[j]
 
             @pl.when(jnp.logical_and(b >= 0, b < blocks))
@@ -387,14 +399,14 @@
 
         return carry
 
-    lax.fori_loop(0, blocks + LAG[3], tick, 0)
+    lax.fori_loop(0, blocks + LAG[2], tick, 0)
 
     def drain(b, carry):
         for d in range(4):
             pair_copy(b, d).wait_send()
-        for j in range(3):
-            for way in range(2):
-                ring_copy(b, j, way).wait_send()
+        for way in range(2):
+            half_copy(b, way).wait_send()
+            full_copy(b, way).wait_send()
         return carry
 
     lax.fori_loop(0, blocks, drain, 0)
@@ -419,9 +431,12 @@
             pltpu.VMEM((blocks, 4, Q, feat), F32),
             pltpu.VMEM((blocks, 4, Q, feat), BF16),
             pltpu.VMEM((blocks, 4, Q, feat), BF16),
-            pltpu.VMEM((blocks, 3, 2, Q // 2, feat), BF16),
-            pltpu.VMEM((blocks, 3, 2, Q // 2, feat), BF16),
-            dma((8,)), dma((blocks, 4)), dma((blocks, 4)), dma((blocks, 3, 2)), dma((blocks, 3, 2)),
+            pltpu.VMEM((blocks, 2, Q // 2, feat), BF16),
+            pltpu.VMEM((blocks, 2, Q // 2, feat), BF16),
+            pltpu.VMEM((blocks, 2, Q, feat), BF16),
+            pltpu.VMEM((blocks, 2, Q, feat), BF16),
+            dma((8,)), dma((blocks, 4)), dma((blocks, 4)),
+            dma((blocks, 2)), dma((blocks, 2)), dma((blocks, 2)), dma((blocks, 2)),
         ],
         compiler_params=pltpu.CompilerParams(
             collective_id=2, has_side_effects=True, vmem_limit_bytes=VMEM_LIMIT

time: 160 us -> 157 us (0.981)
  Pallas kernels: 136 us -> 133 us
    pallas_call x1, Pallas kernels: 55.4 us -> 53.6 us  [project(): pl.pallas_call(project_kernel, in_specs=[vmem] * 5 + [pl.BlockSpec(memory...]
where the time goes in v6:
time: 157 us; the launch traced here: 156 us
  Pallas kernels  133 us (85%)
  between operations  13.5 us (9%)
  local copies, waits for them, and re-layouts  4.62 us (3%)
  starting transfers between devices  3.91 us (2%)
    pallas_call x1, Pallas kernels, project(): pl.pallas_call(project_kernel, in_specs=[vmem] * 5 + [pl.BlockSpec(memory...  53.6 us
    pallas_call x1, Pallas kernels, exchange(): pl.pallas_call(functools.partial(exchange_kernel, chunks=chunks), in_spec...  35.8 us
    pallas_call x1, Pallas kernels, local_scan(): pl.pallas_call(scan_kernel, grid=(tokens // Q,), in_specs=[smem, smem, ro...  20.1 us
    pallas_call x1, Pallas kernels, lowrank(): pl.pallas_call(lowrank_kernel, in_specs=[pl.BlockSpec(memory_space=pltpu....  12.1 us
    pallas_call x1, Pallas kernels, lay_out(): pl.pallas_call(lay_out_kernel, grid_spec=pltpu.PrefetchScalarGridSpec(num...  7.18 us
    pallas_call x1, Pallas kernels, adapt(): pl.pallas_call(adapt_kernel, grid_spec=pltpu.PrefetchScalarGridSpec(num_s...  4.31 us
    ppermute x1, starting transfers between devices, local(): halo = lax.ppermute(tails, 'ctx', [(i, i + 1) for i in range(count - 1)])  3.91 us
    unnamed x12, local copies, waits for them, and re-layouts  3.27 us
  transfers between devices with their start and end apart: 2, of which 1 were waited for; matrix products, arithmetic and copies ran while one was open for 0% of the time, Pallas kernels for 70%

profile of v6, /device:TPU:0, one launch (start us, length us, event | category | flops | bytes accessed | tf_op | source)
XLA Modules:
  0.0 156.0 jit_solution(9207166770877821415)
XLA Ops:
  6.5 0.0 reduce-scatter.4.cloned.1.call-start
  6.5 7.2 %lay_out.1 = bf16[48,64,1536]{2,1,0:T(8,128)(2,1)} custom-call(s32[32]{0:T(128)} %tenant_ref.1, s32[96]{0:T(128)} %index_ref.1, bf16[6,64,1024]{2,1,0:T(8,128)(2,1)} %bitcast.2, bf16[6,64,512]{2,1,0:T(8,128)(2,1)} %up_ref.1), custom_call_target="tpu_custom_call" | custom-call | tf_op jit(solution)/shard_map/lay_out/pallas_call | solution.py:560
  13.7 0.0 slice-start
  13.7 0.0 slice-start.1
  13.7 0.0 slice-start.2
  13.7 0.0 copy-start.5
  13.7 0.0 copy-start.4
  13.7 0.0 reduce-scatter.4.cloned.1.call-update
  13.8 0.7 slice-done
  14.4 0.0 slice-done.1
  14.4 0.0 slice-done.2
  14.4 3.9 %collective-permute-start = (bf16[8,1280]{1,0:T(8,128)(2,1)S(1)}, bf16[8,1280]{1,0:T(8,128)(2,1)S(1)}, u32[]{:S(2)}, u32[]{:S(2)}) collective-permute-start(bf16[8,1280]{1,0:T(8,128)(2,1)S(1)} %pad_maximum_fusion), channel_id=1, source_target_pairs={{0,8},{8,16},{16,24},{24,32},{32,40},{40,48},{48,56},{56,64},{64,7... | collective-permute-start | bytes 61448 | tf_op jit(solution)/shard_map/ppermute | solution.py:637
  18.4 0.0 copy-done.5
  18.4 0.1 dynamic_slice.3
  18.5 0.1 fusion.slot_ref
  18.5 0.0 copy-done.4
  18.5 0.6 reshape.9.gain_ref
  19.1 0.7 collective-permute-done.halo_ref
  19.8 0.0 copy-start.3
  19.8 0.6 copy-done.3
  20.4 20.1 %local_scan.1 = (bf16[1024,1024]{1,0:T(8,128)(2,1)}, bf16[1024,1024]{1,0:T(8,128)(2,1)}, bf16[1024,128]{1,0:T(8,128)(2,1)}, f32[128,1024]{1,0:T(8,128)}, f32[8,1024]{1,0:T(8,128)}) custom-call(f32[16]{0:T(128)} %rate_ref.1, f32[16]{0:T(128)} %skip_ref.1, bf16[1024,1024]{1,0:T(8,128)(2,1)} %x_ref.1, bf16[1024,128]{1,0:T(8,128)(2,1)} %b_ref.1, ...), custom_call_target="tpu_custom_call" | custom-call | tf_op jit(solution)/shard_map/local_scan/pallas_call | solution.py:141
  40.5 35.8 %state_exchange.1.inc_ref = bf16[128,1024]{1,0:T(8,128)(2,1)} custom-call(f32[128,1024]{1,0:T(8,128)} %get-tuple-element.17.s_ref, f32[8,1024]{1,0:T(8,128)} %get-tuple-element.18.d_ref), custom_call_target="tpu_custom_call" | custom-call | tf_op jit(solution)/shard_map/state_exchange/pallas_call | solution.py:262
  76.4 53.6 %project.1 = (f32[1024,512]{1,0:T(8,128)}, bf16[1024,1024]{1,0:T(8,128)(2,1)}) custom-call(bf16[1024,1024]{1,0:T(8,128)(2,1)} %get-tuple-element.14.ylg_ref, bf16[1024,1024]{1,0:T(8,128)(2,1)} %get-tuple-element.15.eg_ref, bf16[1024,128]{1,0:T(8,128)(2,1)} %get-tuple-element.16.cc_ref, bf16[128,1024]{1,0:T(8,128)(2,1)} %state_exchange.1.inc_ref, ...), custom_call_target="tpu_custom_call" | custom-call | tf_op jit(solution)/shard_map/project/pallas_call | solution.py:421
  130.0 0.0 reduce-scatter.4.cloned.1.call-done.panel_ref.up_ref
  130.0 0.0 copy-start
  130.0 1.1 copy-done
  131.1 0.0 copy-start.2
  131.1 1.6 %copy-done.2 = bf16[1024,1024]{1,0:T(8,128)(2,1)S(1)} copy-done((bf16[1024,1024]{1,0:T(8,128)(2,1)S(1)}, bf16[1024,1024]{1,0:T(8,128)(2,1)}, u32[]{:S(2)}) %copy-start.2) | copy-done | bytes 2097176
  132.6 0.0 copy-start.1
  132.7 12.1 %lowrank.1.low_ref = bf16[8,64,128]{2,1,0:T(8,128)(2,1)S(1)} custom-call(s32[8]{0:T(128)S(1)} %fusion.slot_ref, bf16[1024,1024]{1,0:T(8,128)(2,1)S(1)} %copy-done.2, bf16[3,64,1536]{2,1,0:T(8,128)(2,1)S(1)} %copy-done), custom_call_target="tpu_custom_call" | custom-call | tf_op jit(solution)/shard_map/lowrank/pallas_call | solution.py:528
  144.8 0.0 copy-done.1
  144.8 4.3 %adapt.1 = bf16[1024,512]{1,0:T(8,128)(2,1)} custom-call(s32[8]{0:T(128)S(1)} %fusion.slot_ref, f32[1024,512]{1,0:T(8,128)S(1)} %copy-done.1, bf16[8,64,128]{2,1,0:T(8,128)(2,1)S(1)} %lowrank.1.low_ref, bf16[3,64,1536]{2,1,0:T(8,128)(2,1)S(1)} %copy-done), custom_call_target="tpu_custom_call" | custom-call | tf_op jit(solution)/shard_map/adapt/pallas_call | solution.py:583
  (2 shorter events, 0.0 us)
Async XLA Ops:
  6.5 123.4 %reduce-scatter.4.cloned.1.call-start = ((), (), s32[]{:S(2)}) async-start(), calls=%async_computation.1 | async-start | bytes 10027008
  13.7 0.7 slice-start
  13.7 0.7 slice-start.1
  13.7 0.7 slice-start.2
  13.7 4.6 %copy-start.5 = (s32[32]{0:T(128)S(1)}, s32[32]{0:T(128)}, u32[]{:S(2)}) copy-start(s32[32]{0:T(128)} %param.31) | copy-start | bytes 388
  13.7 4.8 %copy-start.4 = (bf16[1024]{0:T(1024)(128)(2,1)S(1)}, bf16[1024]{0:T(1024)(128)(2,1)}, u32[]{:S(2)}) copy-start(bf16[1024]{0:T(1024)(128)(2,1)} %param.27) | copy-start | bytes 6148
  14.4 5.4 %collective-permute-start = (bf16[8,1280]{1,0:T(8,128)(2,1)S(1)}, bf16[8,1280]{1,0:T(8,128)(2,1)S(1)}, u32[]{:S(2)}, u32[]{:S(2)}) collective-permute-start(bf16[8,1280]{1,0:T(8,128)(2,1)S(1)} %pad_maximum_fusion), channel_id=1, source_target_pairs={{0,8},{8,16},{16,24},{24,32},{32,40},{40,48},{48,56},{56,64},{64,7... | collective-permute-start | bytes 61448 | tf_op jit(solution)/shard_map/ppermute | solution.py:637
  19.8 0.6 copy-start.3
  130.0 1.1 copy-start
  131.1 1.6 %copy-start.2 = (bf16[1024,1024]{1,0:T(8,128)(2,1)S(1)}, bf16[1024,1024]{1,0:T(8,128)(2,1)}, u32[]{:S(2)}) copy-start(bf16[1024,1024]{1,0:T(8,128)(2,1)} %get-tuple-element.21.normed_ref) | copy-start | bytes 6291460
  132.6 12.2 %copy-start.1 = (f32[1024,512]{1,0:T(8,128)S(1)}, f32[1024,512]{1,0:T(8,128)}, u32[]{:S(2)}) copy-start(f32[1024,512]{1,0:T(8,128)} %get-tuple-element.19.base_ref) | copy-start | bytes 6291460
Sparse Core Ops, SparseCore 0:
  13.9 96.7 reduce-scatter.3
